TPU v7x, 512 devices: a whole 4x8x8 slice. The times are simulated.
512 devices in a mesh: rows: 256 (over z, x, y), modes: 2 (over core).
Axes of the slice: x: 4, y: 8, z: 8, core: 2. Of those that a mesh axis runs over, the one named last changes fastest.
Arguments:
- sample_rows: int32 [256], replicated, may hold values from 0 to 524287, as said below
- basis: float32 [524288, 256], P('rows', 'modes')
- snapshots: float32 [524288, 128], P('rows', 'modes')
Outputs:
- projector: float32 [524288, 256], P('rows', 'modes')
- residual: float32 [524288, 128], P('rows', 'modes')
- residual_rms: float32 [128], P('modes')
Inputs may be any that keep to these rules, and one draw needn't show every extreme that they name: `sample_rows`: the indices are distinct. No slab of 2048 consecutive rows (rows j * 2048 to (j + 1) * 2048 - 1) holds more than 8 of them, and some slab holds exactly 8. sampled is row-wise diagonally dominant.
All inputs are finite; a program needn't handle non-finite values.
Results may differ from a plain program's by a relative error of at most 0.000084.
Values sent between devices are 32-bit elements; how exact they have to be, the bound alone decides.
No kernel may reach another device: no remote copies, remote signals or barrier semaphores. Data moves between devices by JAX's collectives and lax.ppermute only.
A program may use at most 128 MiB of HBM per device.

v0:
```python
import jax
import jax.numpy as jnp
from jax import lax
from jax.sharding import Mesh
from jax.sharding import PartitionSpec as P

ROWS = ("rows_0", "rows_1", "rows_2")


def in_one_piece(arrays, axis, dim, along):
    ends, at = ([], 0)
    for a in arrays[:-1]:
        at += a.shape[along]
        ends.append(at)
    both = jnp.concatenate(arrays, axis=along)
    return tuple(jnp.split(lax.all_gather(both, axis, axis=dim, tiled=True), ends, axis=along))


def laid_out(tiles, dim):
    tiles = jnp.moveaxis(tiles, 0, dim)
    lengths = tiles.shape
    return tiles.reshape(*lengths[:dim], lengths[dim] * lengths[dim + 1], *lengths[dim + 2 :])


def copy_for_each(value, axis):
    peers = lax.axis_size(axis)
    return lax.all_to_all(
        jnp.broadcast_to(value[None], (peers, *value.shape)), axis, 0, 0, tiled=True
    )


def collect(value, axis, dim):
    return laid_out(copy_for_each(value, axis), dim)


def one_axis_at_a_time(value, axes):
    for axis in axes:
        value = lax.psum(value, axis)
    return value


def matmul(left, right):
    return jnp.dot(left, right, precision=lax.Precision.HIGHEST)


def invert(matrix):
    order = matrix.shape[0]
    if order <= 8:
        current = matrix
        result = jnp.eye(order, dtype=matrix.dtype)
        for pivot in range(order):
            scale = 1.0 / current[pivot, pivot]
            pivot_row = current[pivot] * scale
            result_row = result[pivot] * scale
            column = current[:, pivot].at[pivot].set(0.0)
            current = current - column[:, None] * pivot_row[None, :]
            result = result - column[:, None] * result_row[None, :]
            current = current.at[pivot].set(pivot_row)
            result = result.at[pivot].set(result_row)
        return result
    half_n = order // 2
    top_inv = invert(matrix[:half_n, :half_n])
    upper_right = matrix[:half_n, half_n:]
    lower_left = matrix[half_n:, :half_n]
    left_solved = matmul(lower_left, top_inv)
    right_solved = matmul(top_inv, upper_right)
    schur_inv = invert(matrix[half_n:, half_n:] - matmul(lower_left, right_solved))
    corner_right = -matmul(right_solved, schur_inv)
    corner_left = -matmul(schur_inv, left_solved)
    corner_top = top_inv - matmul(corner_right, left_solved)
    upper_band = jnp.concatenate([corner_top, corner_right], axis=1)
    lower_band = jnp.concatenate([corner_left, schur_inv], axis=1)
    return jnp.concatenate([upper_band, lower_band], axis=0)


def on_device(sample_rows, basis, snapshots):
    slab_rows = basis.shape[0]
    modes_half = basis.shape[1]
    count = sample_rows.shape[0]
    first_row = lax.axis_index(ROWS) * slab_rows
    local_rows = sample_rows - first_row
    positions = jnp.arange(slab_rows, dtype=jnp.int32)
    devices = lax.axis_size(ROWS)
    capacity = max(8, 2 * count // devices)
    owner = sample_rows // slab_rows
    earlier = (owner[None, :] == owner[:, None]) & (sample_rows[None, :] < sample_rows[:, None])
    slot_rank = jnp.sum(earlier.astype(jnp.int32), axis=1)
    owned_rows = (local_rows >= 0) & (local_rows < slab_rows)
    slot_ids = jnp.arange(capacity, dtype=jnp.int32)
    slot_hit = owned_rows[None, :] & (slot_rank[None, :] == slot_ids[:, None])
    slot_local = jnp.sum(jnp.where(slot_hit, local_rows[None, :], 0), axis=1)
    slot_used = jnp.any(slot_hit, axis=1)
    selector = ((slot_local[:, None] == positions[None, :]) & slot_used[:, None]).astype(
        jnp.float32
    )
    packed_basis = matmul(selector, basis)
    packed_snaps = matmul(selector, snapshots)
    all_basis, all_snaps = in_one_piece((packed_basis, packed_snaps), ROWS, 0, 1)
    slot_global = owner * capacity + slot_rank
    table_ids = jnp.arange(devices * capacity, dtype=jnp.int32)
    picker = (slot_global[:, None] == table_ids[None, :]).astype(jnp.float32)
    sampled_half = matmul(picker, all_basis)
    picked = matmul(picker, all_snaps)
    sampled = lax.all_gather(sampled_half, "modes", axis=1, tiled=True)
    inverse = invert(sampled)
    first_col = lax.axis_index("modes") * modes_half
    inverse_cols = lax.dynamic_slice_in_dim(inverse, first_col, modes_half, 1)
    coeffs = matmul(inverse, picked)
    solved = jnp.concatenate([inverse_cols, coeffs], axis=1)
    products = matmul(collect(basis, "modes", 1), solved)
    projector = products[:, :modes_half]
    residual = snapshots - products[:, modes_half:]
    squares = one_axis_at_a_time(jnp.sum(residual * residual, axis=0), ROWS)
    total_rows = slab_rows * lax.axis_size(ROWS)
    residual_rms = jnp.sqrt(squares / total_rows)
    return (projector, residual, residual_rms)


def solution(mesh):
    torus = Mesh(
        mesh.devices.reshape(8, 4, 8, mesh.shape["modes"]), ("rows_0", "rows_1", "rows_2", "modes")
    )
    return jax.shard_map(
        on_device,
        mesh=torus,
        in_specs=(P(), P(ROWS, "modes"), P(ROWS, "modes")),
        out_specs=(P(ROWS, "modes"), P(ROWS, "modes"), P("modes")),
        check_vma=False,
    )
```

profile of v0, /device:TPU:8, one launch (start us, length us, event | category | flops | bytes accessed | tf_op | source)
XLA Modules:
  0.0 659.9 jit_solution(15293892479721838865)
XLA Ops:
  7.2 0.8 and_select_fusion
  8.0 1.0 convert_reduce_fusion
  9.9 1.4 fusion.12
  11.3 1.7 fusion.14
  14.0 1.5 broadcast_in_dim.16
  15.5 3.9 all-to-all-start
  19.5 115.6 %all-gather.2.cloned.1.call-done = f32[2048,192]{1,0:T(8,128)} async-done(((f32[8,192]{1,0:T(8,128)}), f32[2048,192]{1,0:T(8,128)}) %all-gather.2.cloned.1.call-update) | async-done | bytes 1572880 | tf_op jit(solution)/shard_map/all_gather | solution.py:16
  135.1 2.4 fusion.1
  137.5 2.0 all_gather.7
  143.0 1.2 constant_dynamic-update-slice_fusion.255
  144.2 0.7 multiply_subtract_fusion.430
  147.0 1.2 constant_dynamic-update-slice_fusion.223
  148.2 0.7 multiply_subtract_fusion.428
  151.0 1.2 constant_dynamic-update-slice_fusion.191
  154.9 1.2 constant_dynamic-update-slice_fusion.159
  158.9 1.2 constant_dynamic-update-slice_fusion.127
  162.8 1.2 constant_dynamic-update-slice_fusion.95
  605.5 1.2 fusion
  607.1 1.5 convolution_bitcast_fusion
  608.7 1.0 multiply_reduce_fusion
  609.7 1.3 copy.113
  611.0 15.9 %psum.21 = f32[64]{0:T(128)S(1)} all-reduce(f32[64]{0:T(128)S(1)} %get-tuple-element.8844), channel_id=1, replica_groups=mesh['rows_0'=8,'rows_1'=4,'rows_2'=8,'modes'=2] {'rows_0'}, use_global_device_ids=true, to_apply=%region_4.5 | all-reduce | flops 64 | bytes 512 | tf_op jit(solution)/shard_map/psum | solution.py:38
  626.9 10.2 %psum.22 = f32[64]{0:T(128)S(1)} all-reduce(f32[64]{0:T(128)S(1)} %psum.21), channel_id=1, replica_groups=mesh['rows_0'=8,'rows_1'=4,'rows_2'=8,'modes'=2] {'rows_1'}, use_global_device_ids=true, to_apply=%region_5.6 | all-reduce | flops 64 | bytes 512 | tf_op jit(solution)/shard_map/psum | solution.py:38
  637.1 15.0 %psum.23 = f32[64]{0:T(128)S(1)} all-reduce(f32[64]{0:T(128)S(1)} %psum.22), channel_id=1, replica_groups=mesh['rows_0'=8,'rows_1'=4,'rows_2'=8,'modes'=2] {'rows_2'}, use_global_device_ids=true, to_apply=%region_6.7 | all-reduce | flops 64 | bytes 512 | tf_op jit(solution)/shard_map/psum | solution.py:38
  (2669 shorter events, 276.4 us)
Async XLA Ops:
  7.2 6.5 copy-start
  7.2 127.9 %all-gather.2.cloned.1.call-start = ((), (), s32[]{:S(2)}) async-start(), calls=%async_computation.1 | async-start | bytes 2105344 | tf_op jit(solution)/shard_map/all_gather | solution.py:16
  15.5 3.9 copy-start.3
  15.5 591.6 %all-to-all-start = ((f32[2,2048,128]{1,2,0:T(8,128)}), f32[2,2048,128]{1,2,0:T(8,128)S(1)}, u32[]{:S(2)}, u32[]{:S(2)}) async-start(f32[2,2048,128]{1,2,0:T(8,128)} %broadcast_in_dim.16), calls=%async_computation | async-start | bytes 4194304 | tf_op jit(solution)/shard_map/all_to_all | solution.py:27
  602.4 3.2 copy-start.2
  607.1 1.6 copy-start.1
Sparse Core Ops, SparseCore 0:
  13.8 121.2 all-gather.1
where the time goes:
time: 671 us; the launch traced here: 660 us
  local copies, waits for them, and re-layouts  226 us (34%)
  between operations  199 us (30%)
  waiting for transfers between devices  116 us (17%)
  blocking collectives  43.1 us (6%)
  matrix products  38.2 us (6%)
  other arithmetic  34.2 us (5%)
    slice x256, local copies, waits for them, and re-layouts, invert(): scale = 1.0 / current[pivot, pivot]  149 us
    all_gather x1, waiting for transfers between devices, in_one_piece(): lax.all_gather(both, axis, axis=dim, tiled=True)  116 us
    slice x256, local copies, waits for them, and re-layouts, invert(): column = current[:, pivot].at[pivot].set(0.0)  47.6 us
    psum x3, blocking collectives, one_axis_at_a_time(): value = lax.psum(value, axis)  41.1 us
    dot_general x192, matrix products, matmul(): return jnp.dot(left, right, precision=lax.Precision.HIGHEST)  38.2 us
    sub x224, other arithmetic, invert(): current = current - column[:, None] * pivot_row[None, :]  20.6 us
  transfers between devices with their start and end apart: 2, of which 1 were waited for; matrix products, arithmetic and copies ran while one was open for 44% of the time, Pallas kernels for 0%

commit v1 on v0

v1 whole, which is shorter than its diff:
```python
import functools

import jax
import jax.numpy as jnp
from jax import lax
from jax.experimental import pallas as pl
from jax.experimental.pallas import tpu as pltpu
from jax.sharding import Mesh
from jax.sharding import PartitionSpec as P

ROWS = ("rows_0", "rows_1", "rows_2")
F32 = jnp.float32
BF16 = jnp.bfloat16
NT = (((1,), (1,)), ((), ()))
DOUBLINGS = 5
REFINES = 3
TILE = 256
MOST = 8


def dot_once(left, right):
    return jnp.dot(left.astype(BF16), right.astype(BF16), preferred_element_type=F32)

def dot_full(left, right):
    return jnp.dot(left, right, precision=lax.Precision.HIGHEST, preferred_element_type=F32)

def eliminate(matrix, right):
    order, width = matrix.shape
    lanes = lax.broadcasted_iota(jnp.int32, (order, width), 1)
    places = lax.broadcasted_iota(jnp.int32, (order, 1), 0)
    lane = lax.broadcasted_iota(jnp.int32, (1, width), 1)
    def step(k, carry):
        row = matrix[pl.ds(k, 1), :]
        scale = 1.0 / jnp.sum(jnp.where(lane == k, row, 0.0), axis=1, keepdims=True)
        row = row * scale
        answer = right[pl.ds(k, 1), :] * scale
        column = jnp.sum(jnp.where(lanes == k, matrix[...], 0.0), axis=1, keepdims=True)
        column = jnp.where(places == k, 0.0, column)
        matrix[...] = matrix[...] - column * row
        right[...] = right[...] - column * answer
        matrix[pl.ds(k, 1), :] = row
        right[pl.ds(k, 1), :] = answer
        return carry
    lax.fori_loop(0, order, step, 0)

def solve(sampled, right, matrix, answer):
    order = sampled.shape[0]
    i = lax.broadcasted_iota(jnp.int32, (order, order), 0)
    j = lax.broadcasted_iota(jnp.int32, (order, order), 1)
    eye = i == j
    scale = 1.0 / jnp.sum(jnp.where(eye, sampled, 0.0), axis=1, keepdims=True)
    scaled = jnp.where(eye, 1.0, sampled * scale)
    right = right * scale
    power = jnp.where(eye, 0.0, -scaled)
    guess = jnp.where(eye, 1.0, power)
    for _ in range(DOUBLINGS):
        low = power.astype(BF16)
        power = jnp.dot(low, low, preferred_element_type=F32)
        guess = guess + dot_once(power, guess)
    guess = guess.astype(BF16)
    out = jnp.dot(guess, right.astype(BF16), preferred_element_type=F32)
    for _ in range(REFINES):
        fix = jnp.dot(guess, (right - dot_full(scaled, out)).astype(BF16), preferred_element_type=F32)
        out = out + fix
    answer[...] = out
    size = jnp.max(jnp.abs(out), axis=0, keepdims=True)
    change = jnp.max(jnp.abs(fix), axis=0, keepdims=True)
    settled = jnp.min(jnp.where(change <= 1e-4 * size, 1.0, 0.0))
    @pl.when(settled < 0.5)
    def _():
        matrix[...] = scaled
        answer[...] = right
        eliminate(matrix, answer)

def finish_body(table, swapped, own, other, snaps, projector, residual, squares,
                modes_v, snaps_v, projector_v, residual_v, matrix, answer, sem_in, sem_out):
    rows, half = own.shape
    mode = lax.axis_index("modes")
    mine = pl.ds(pl.multiple_of(mode * half, half), half)
    theirs = pl.ds(pl.multiple_of((1 - mode) * half, half), half)
    loads = [
        pltpu.make_async_copy(own, modes_v.at[:, mine], sem_in.at[0]),
        pltpu.make_async_copy(other, modes_v.at[:, theirs], sem_in.at[1]),
        pltpu.make_async_copy(snaps, snaps_v, sem_in.at[2]),
    ]
    for load in loads:
        load.start()
    shape = (table.shape[0], table.shape[2])
    here, there = table[...].reshape(shape), swapped[...].reshape(shape)
    first = jnp.where(mode == 0, here[:, :half], there[:, :half])
    second = jnp.where(mode == 0, there[:, :half], here[:, :half])
    sampled = jnp.concatenate([first, second], axis=1)
    picked = here[:, half:]
    order = sampled.shape[0]
    i = lax.broadcasted_iota(jnp.int32, (order, half), 0)
    j = lax.broadcasted_iota(jnp.int32, (order, half), 1)
    columns = jnp.where(i == j + mode * half, 1.0, 0.0)
    solve(sampled, jnp.concatenate([columns, picked], axis=1), matrix, answer)
    for load in loads:
        load.wait()
    solved = answer[...]
    total = jnp.zeros((snaps.shape[0], TILE), F32)
    stores = []
    for at in range(0, rows, TILE):
        tile = pl.ds(at, TILE)
        product = dot_full(modes_v[tile, :], solved)
        projector_v[tile, :] = product[:, :half]
        left = snaps_v[:, tile] - product[:, half:].T
        residual_v[:, tile] = left
        total = total + left * left
        n = at // TILE
        stores += [
            pltpu.make_async_copy(projector_v.at[tile, :], projector.at[tile, :], sem_out.at[0, n]),
            pltpu.make_async_copy(residual_v.at[:, tile], residual.at[:, tile], sem_out.at[1, n]),
        ]
        stores[-2].start()
        stores[-1].start()
    sums = lax.dot_general(
        jnp.ones((8, TILE), F32), total, NT,
        precision=lax.Precision.HIGHEST, preferred_element_type=F32,
    )
    squares[...] = jnp.broadcast_to(sums[0:1][None], squares.shape)
    for store in stores:
        store.wait()

def finish(table, swapped, own, other, snaps):
    rows, half = own.shape
    shots = snaps.shape[0]
    order = table.shape[0]
    anyspace = pl.BlockSpec(memory_space=pl.ANY)
    vm = pl.BlockSpec(memory_space=pltpu.VMEM)
    return pl.pallas_call(
        finish_body,
        out_shape=(jax.ShapeDtypeStruct((rows, half), F32), jax.ShapeDtypeStruct((shots, rows), F32),
                   jax.ShapeDtypeStruct((order, 1, shots), F32)),
        in_specs=[vm, vm, anyspace, anyspace, anyspace],
        out_specs=(anyspace, anyspace, vm),
        scratch_shapes=[
            pltpu.VMEM((rows, 2 * half), F32), pltpu.VMEM((shots, rows), F32),
            pltpu.VMEM((rows, half), F32), pltpu.VMEM((shots, rows), F32),
            pltpu.VMEM((order, order), F32), pltpu.VMEM((order, half + shots), F32),
            pltpu.SemaphoreType.DMA((3,)), pltpu.SemaphoreType.DMA((2, rows // TILE)),
        ],
        compiler_params=pltpu.CompilerParams(vmem_limit_bytes=32 * 1024 * 1024),
        cost_estimate=pl.CostEstimate(flops=2*rows*256*192, bytes_accessed=6*1024*1024, transcendentals=0),
        name="finish",
    )(table, swapped, own, other, snaps)


def pick_body(sizes, wanted, basis, snaps, table, blocks, strips, staged, place, found, sem):
    rows = basis.shape[0]
    count = table.shape[0]
    half = basis.shape[1]
    slab = 0
    for axis, size in zip(ROWS, sizes):
        slab = slab * size + lax.axis_index(axis)
    start = slab * rows

    def copies(slot, row):
        block = pl.ds(pl.multiple_of(row // 8 * 8, 8), 8)
        strip = pl.ds(pl.multiple_of(row // 128 * 128, 128), 128)
        return (
            pltpu.make_async_copy(basis.at[block, :], blocks.at[slot], sem.at[0, slot]),
            pltpu.make_async_copy(snaps.at[:, strip], strips.at[slot], sem.at[1, slot]),
        )

    for slot in range(MOST):
        found[slot] = 0
        place[slot] = 0

    def look(i, slot):
        row = wanted[i] - start
        held = (row >= 0) & (row < rows) & (slot < MOST)

        @pl.when(held)
        def _():
            found[slot] = row
            place[slot] = i
            for copy in copies(slot, row):
                copy.start()

        return slot + held.astype(jnp.int32)

    used = lax.fori_loop(0, count, look, 0, unroll=8)
    table[...] = jnp.zeros(table.shape, F32)
    for slot in range(MOST):

        @pl.when(slot < used)
        def _():
            for copy in copies(slot, found[slot]):
                copy.wait()

    lanes = lax.broadcasted_iota(jnp.int32, (8, 128), 1)
    for slot in range(MOST):
        row = found[slot]
        hit = jnp.where(lanes == row % 128, 1.0, 0.0)
        shots = lax.dot_general(
            hit, strips[slot], NT, precision=lax.Precision.HIGHEST, preferred_element_type=F32
        )
        staged[slot, :, :half] = blocks[slot, pl.ds(row % 8, 1), :]
        staged[slot, :, half:] = shots[0:1]
    for slot in range(MOST):

        @pl.when(slot < used)
        def _():
            table[pl.ds(place[slot], 1)] = staged[pl.ds(slot, 1)]


def pick(sizes, wanted, basis, snaps):
    half, shots = basis.shape[1], snaps.shape[0]
    anywhere = pl.BlockSpec(memory_space=pl.ANY)
    return pl.pallas_call(
        functools.partial(pick_body, sizes),
        out_shape=jax.ShapeDtypeStruct((wanted.shape[0], 1, half + shots), F32),
        in_specs=[pl.BlockSpec(memory_space=pltpu.SMEM), anywhere, anywhere],
        out_specs=pl.BlockSpec(memory_space=pltpu.VMEM),
        scratch_shapes=[
            pltpu.VMEM((MOST, 8, half), F32),
            pltpu.VMEM((MOST, shots, 128), F32),
            pltpu.VMEM((MOST, 1, half + shots), F32),
            pltpu.SMEM((MOST,), jnp.int32),
            pltpu.SMEM((MOST,), jnp.int32),
            pltpu.SemaphoreType.DMA((2, MOST)),
        ],
        compiler_params=pltpu.CompilerParams(vmem_limit_bytes=60 * 1024 * 1024),
        name="pick",
    )(wanted, basis, snaps)


def share_body(parts, copies):
    copies[...] = jnp.broadcast_to(jnp.sum(parts[...], axis=0, keepdims=True), copies.shape)


def share(parts):
    inside = pl.BlockSpec(memory_space=pltpu.VMEM)
    return pl.pallas_call(
        share_body,
        out_shape=jax.ShapeDtypeStruct(parts.shape, F32),
        in_specs=[inside],
        out_specs=inside,
        compiler_params=pltpu.CompilerParams(vmem_limit_bytes=8 * 1024 * 1024),
        name="share",
    )(parts)


def root_mean_body(total_rows, squares, out):
    out[...] = jnp.sqrt(jnp.sum(squares[...], axis=0) / total_rows)


def root_mean(squares, total_rows):
    inside = pl.BlockSpec(memory_space=pltpu.VMEM)
    return pl.pallas_call(
        functools.partial(root_mean_body, total_rows),
        out_shape=jax.ShapeDtypeStruct((1, squares.shape[2]), F32),
        in_specs=[inside],
        out_specs=inside,
        compiler_params=pltpu.CompilerParams(vmem_limit_bytes=8 * 1024 * 1024),
        name="root_mean",
    )(squares)


def exchange(blocks):
    return lax.all_to_all(blocks, ROWS, 0, 0, tiled=True)


def on_device(sizes, sample_rows, basis, snapshots):
    snaps = snapshots.T
    other = lax.ppermute(basis, "modes", [(0, 1), (1, 0)])
    parts = exchange(pick(sizes, sample_rows, basis, snaps))
    table = exchange(share(parts))
    swapped = lax.ppermute(table, "modes", [(0, 1), (1, 0)])
    projector, residual, squares = finish(table, swapped, basis, other, snaps)
    total_rows = basis.shape[0] * lax.axis_size(ROWS)
    residual_rms = root_mean(exchange(squares), total_rows)
    return (projector, residual.T, residual_rms.reshape(-1))


def solution(mesh):
    sizes = (8, 4, 8)
    torus = Mesh(mesh.devices.reshape(*sizes, mesh.shape["modes"]), (*ROWS, "modes"))
    return jax.shard_map(
        functools.partial(on_device, sizes),
        mesh=torus,
        in_specs=(P(), P(ROWS, "modes"), P(ROWS, "modes")),
        out_specs=(P(ROWS, "modes"), P(ROWS, "modes"), P("modes")),
        check_vma=False,
    )
```

time: 671 us -> 106 us (0.16)
  the two profiles are of different devices: /device:TPU:8 before, /device:TPU:1 now
where the time goes in v1:
time: 106 us; the launch traced here: 105 us
  blocking collectives  75.3 us (71%)
  Pallas kernels  14.3 us (13%)
  starting transfers between devices  13.9 us (13%)
  waiting for transfers between devices  1.14 us (1%)
    all_to_all x3, blocking collectives, exchange(): return lax.all_to_all(blocks, ROWS, 0, 0, tiled=True)  75.3 us
    ppermute x1, starting transfers between devices, on_device(): other = lax.ppermute(basis, 'modes', [(0, 1), (1, 0)])  8.75 us
    pallas_call x1, Pallas kernels, finish(): pl.pallas_call(finish_body, out_shape=(jax.ShapeDtypeStruct((rows, half),...  6.89 us
    pallas_call x1, Pallas kernels, pick(): pl.pallas_call(functools.partial(pick_body, sizes), out_shape=jax.ShapeDt...  6.28 us
    ppermute x1, starting transfers between devices, on_device(): swapped = lax.ppermute(table, 'modes', [(0, 1), (1, 0)])  5.16 us
  transfers between devices with their start and end apart: 2, of which 1 were waited for; matrix products, arithmetic and copies ran while one was open for 0% of the time, Pallas kernels for 6%

profile of v1, /device:TPU:1, one launch (start us, length us, event | category | flops | bytes accessed | tf_op | source)
XLA Modules:
  0.0 105.4 jit_solution(2862714817293325052)
XLA Ops:
  0.6 8.7 %collective-permute-start.1 = (f32[2048,128]{1,0:T(8,128)}, f32[2048,128]{1,0:T(8,128)S(1)}, u32[]{:S(2)}, u32[]{:S(2)}) collective-permute-start(f32[2048,128]{1,0:T(8,128)} %own.1), channel_id=1, source_target_pairs={{0,1},{1,0},{2,3},{3,2},{4,5},{5,4},{6,7},{7,6},{8,9},{9,8},{10,11... | collective-permute-start | bytes 3145736 | tf_op jit(solution)/shard_map/ppermute | solution.py:268
  9.4 0.0 copy-start.1
  9.4 6.3 %pick.1 = f32[256,1,192]{2,1,0:T(1,128)} custom-call(s32[256]{0:T(256)} %wanted.1, f32[2048,128]{1,0:T(8,128)} %own.1, f32[64,2048]{1,0:T(8,128)} %bitcast.3), custom_call_target="tpu_custom_call" | custom-call | tf_op jit(solution)/shard_map/pick/pallas_call | solution.py:212
  15.7 0.0 copy-start
  15.7 32.0 %all_to_all.15.parts = f32[256,1,192]{2,1,0:T(1,128)S(1)} all-to-all(f32[256,1,192]{2,1,0:T(1,128)} %pick.1), channel_id=1, replica_groups=mesh['rows_0'=8,'rows_1'=4,'rows_2'=8,'modes'=2] {'rows_0','rows_1','row..., dimensions={0} | all-to-all | bytes 393216 | tf_op jit(solution)/shard_map/all_to_all | solution.py:263
  47.7 0.3 share.1
  48.1 22.1 %all_to_all.16.table = f32[256,1,192]{2,1,0:T(1,128)S(1)} all-to-all(f32[256,1,192]{2,1,0:T(1,128)S(1)} %share.1), channel_id=1, replica_groups=mesh['rows_0'=8,'rows_1'=4,'rows_2'=8,'modes'=2] {'rows_0','rows_1','row..., dimensions={0} | all-to-all | bytes 393216 | tf_op jit(solution)/shard_map/all_to_all | solution.py:263
  70.2 5.2 %collective-permute-start = (f32[256,1,192]{2,1,0:T(1,128)S(1)}, f32[256,1,192]{2,1,0:T(1,128)S(1)}, u32[]{:S(2)}, u32[]{:S(2)}) collective-permute-start(f32[256,1,192]{2,1,0:T(1,128)S(1)} %all_to_all.16.table), channel_id=1, source_target_pairs={{0,1},{1,0},{2,3},{3,2},{4,5},{5,4},{6,7},{7,6},{8,9},{9,8},{10,11... | collective-permute-start | bytes 589832 | tf_op jit(solution)/shard_map/ppermute | solution.py:271
  75.4 1.1 %collective-permute-done.swapped = f32[256,1,192]{2,1,0:T(1,128)S(1)} collective-permute-done((f32[256,1,192]{2,1,0:T(1,128)S(1)}, f32[256,1,192]{2,1,0:T(1,128)S(1)}, u32[]{:S(2)}, u32[]{:S(2)}) %collective-permute-start) | collective-permute-done | bytes 196640 | tf_op jit(solution)/shard_map/ppermute | solution.py:271
  76.5 0.0 collective-permute-done.1.other
  76.5 0.0 copy-done.1
  76.5 0.0 copy-done
  76.5 6.9 %finish.1 = (f32[2048,128]{1,0:T(8,128)}, f32[64,2048]{1,0:T(8,128)}, f32[256,1,64]{2,1,0:T(1,128)S(1)}) custom-call(f32[256,1,192]{2,1,0:T(1,128)S(1)} %all_to_all.16.table, f32[256,1,192]{2,1,0:T(1,128)S(1)} %collective-permute-done.swapped, f32[2048,128]{1,0:T(8,128)S(1)} %copy-done, f32[2048,128]{1,0:T(8,128)S(1)} %collective-permute-done.1.other, ...), custom_call_target="tpu_custom_call" | custom-call | flops 201326592 | bytes 6291456 | tf_op jit(solution)/shard_map/finish/pallas_call | solution.py:132
  83.4 21.2 %all_to_all.17.squares = f32[256,1,64]{2,1,0:T(1,128)S(1)} all-to-all(f32[256,1,64]{2,1,0:T(1,128)S(1)} %get-tuple-element.8), channel_id=1, replica_groups=mesh['rows_0'=8,'rows_1'=4,'rows_2'=8,'modes'=2] {'rows_0','rows_1','row..., dimensions={0} | all-to-all | bytes 131072 | tf_op jit(solution)/shard_map/all_to_all | solution.py:263
  104.6 0.8 root_mean.1
Async XLA Ops:
  0.6 75.9 %collective-permute-start.1 = (f32[2048,128]{1,0:T(8,128)}, f32[2048,128]{1,0:T(8,128)S(1)}, u32[]{:S(2)}, u32[]{:S(2)}) collective-permute-start(f32[2048,128]{1,0:T(8,128)} %own.1), channel_id=1, source_target_pairs={{0,1},{1,0},{2,3},{3,2},{4,5},{5,4},{6,7},{7,6},{8,9},{9,8},{10,11... | collective-permute-start | bytes 3145736 | tf_op jit(solution)/shard_map/ppermute | solution.py:268
  9.4 67.1 %copy-start.1 = (f32[2048,64]{0,1:T(8,128)S(1)}, f32[2048,64]{0,1:T(8,128)}, u32[]{:S(2)}) copy-start(f32[2048,64]{0,1:T(8,128)} %param.5) | copy-start | bytes 1572868
  15.7 60.8 %copy-start = (f32[2048,128]{1,0:T(8,128)S(1)}, f32[2048,128]{1,0:T(8,128)}, u32[]{:S(2)}) copy-start(f32[2048,128]{1,0:T(8,128)} %own.1) | copy-start | bytes 3145732
  70.2 6.3 %collective-permute-start = (f32[256,1,192]{2,1,0:T(1,128)S(1)}, f32[256,1,192]{2,1,0:T(1,128)S(1)}, u32[]{:S(2)}, u32[]{:S(2)}) collective-permute-start(f32[256,1,192]{2,1,0:T(1,128)S(1)} %all_to_all.16.table), channel_id=1, source_target_pairs={{0,1},{1,0},{2,3},{3,2},{4,5},{5,4},{6,7},{7,6},{8,9},{9,8},{10,11... | collective-permute-start | bytes 589832 | tf_op jit(solution)/shard_map/ppermute | solution.py:271

commit v2 on v1

--- a/solution.py
+++ b/solution.py
@@ -16,6 +16,8 @@
 REFINES = 3
 TILE = 256
 MOST = 8
+NARROW = 64
+PICK_VMEM = 60 * 1024 * 1024
 
 
 def dot_once(left, right):
@@ -72,7 +74,7 @@
         answer[...] = right
         eliminate(matrix, answer)
 
-def finish_body(table, swapped, own, other, snaps, projector, residual, squares,
+def finish_body(modes, swapped, shots, own, other, snaps, projector, residual, squares,
                 modes_v, snaps_v, projector_v, residual_v, matrix, answer, sem_in, sem_out):
     rows, half = own.shape
     mode = lax.axis_index("modes")
@@ -85,12 +87,11 @@
     ]
     for load in loads:
         load.start()
-    shape = (table.shape[0], table.shape[2])
-    here, there = table[...].reshape(shape), swapped[...].reshape(shape)
-    first = jnp.where(mode == 0, here[:, :half], there[:, :half])
-    second = jnp.where(mode == 0, there[:, :half], here[:, :half])
+    here, there = modes[...], swapped[...]
+    first = jnp.where(mode == 0, here, there)
+    second = jnp.where(mode == 0, there, here)
     sampled = jnp.concatenate([first, second], axis=1)
-    picked = here[:, half:]
+    picked = shots[...]
     order = sampled.shape[0]
     i = lax.broadcasted_iota(jnp.int32, (order, half), 0)
     j = lax.broadcasted_iota(jnp.int32, (order, half), 1)
@@ -123,124 +124,192 @@
     for store in stores:
         store.wait()
 
-def finish(table, swapped, own, other, snaps):
+def finish(modes, swapped, shots, own, other, snaps):
     rows, half = own.shape
-    shots = snaps.shape[0]
-    order = table.shape[0]
+    depth = snaps.shape[0]
+    order = modes.shape[0]
     anyspace = pl.BlockSpec(memory_space=pl.ANY)
     vm = pl.BlockSpec(memory_space=pltpu.VMEM)
     return pl.pallas_call(
         finish_body,
-        out_shape=(jax.ShapeDtypeStruct((rows, half), F32), jax.ShapeDtypeStruct((shots, rows), F32),
-                   jax.ShapeDtypeStruct((order, 1, shots), F32)),
-        in_specs=[vm, vm, anyspace, anyspace, anyspace],
+        out_shape=(jax.ShapeDtypeStruct((rows, half), F32), jax.ShapeDtypeStruct((depth, rows), F32),
+                   jax.ShapeDtypeStruct((order, 1, depth), F32)),
+        in_specs=[vm, vm, vm, anyspace, anyspace, anyspace],
         out_specs=(anyspace, anyspace, vm),
         scratch_shapes=[
-            pltpu.VMEM((rows, 2 * half), F32), pltpu.VMEM((shots, rows), F32),
-            pltpu.VMEM((rows, half), F32), pltpu.VMEM((shots, rows), F32),
-            pltpu.VMEM((order, order), F32), pltpu.VMEM((order, half + shots), F32),
+            pltpu.VMEM((rows, 2 * half), F32), pltpu.VMEM((depth, rows), F32),
+            pltpu.VMEM((rows, half), F32), pltpu.VMEM((depth, rows), F32),
+            pltpu.VMEM((order, order), F32), pltpu.VMEM((order, half + depth), F32),
             pltpu.SemaphoreType.DMA((3,)), pltpu.SemaphoreType.DMA((2, rows // TILE)),
         ],
         compiler_params=pltpu.CompilerParams(vmem_limit_bytes=32 * 1024 * 1024),
         cost_estimate=pl.CostEstimate(flops=2*rows*256*192, bytes_accessed=6*1024*1024, transcendentals=0),
         name="finish",
-    )(table, swapped, own, other, snaps)
-
-
-def pick_body(sizes, wanted, basis, snaps, table, blocks, strips, staged, place, found, sem):
-    rows = basis.shape[0]
-    count = table.shape[0]
-    half = basis.shape[1]
-    slab = 0
+    )(modes, swapped, shots, own, other, snaps)
+
+
+def pick_body(sizes, wanted, basis, snaps, sends, places, crowded, blocks, strips, sem):
+    rows, half = basis.shape
+    shots = snaps.shape[0]
+    count = wanted.shape[1]
+    deep = sizes[1] * sizes[2]
+    start = 0
     for axis, size in zip(ROWS, sizes):
-        slab = slab * size + lax.axis_index(axis)
-    start = slab * rows
-
-    def copies(slot, row):
+        start = start * size + lax.axis_index(axis)
+    start = start * rows
+
+    key = wanted[...]
+    local = key % rows
+    slab = key // rows
+    plane = slab // deep
+    line = slab % deep
+    across = jnp.broadcast_to(key.astype(F32), (count, count))
+    down = across.T
+    before = down < across
+
+    def earlier(first):
+        same = before & (down >= first.astype(F32))
+        return jnp.sum(jnp.where(same, 1.0, 0.0), axis=0, keepdims=True)
+
+    rank = earlier(key - local)
+    place = earlier(plane * deep * rows)
+    slot = (line * MOST).astype(F32) + rank
+    empty = jnp.zeros((8 - 3, count), F32)
+    places[...] = jnp.concatenate([place, plane.astype(F32), slot, empty], axis=0)
+    crowded[0] = (jnp.max(place) >= NARROW).astype(jnp.int32)
+
+    turn = lax.broadcasted_iota(jnp.int32, (MOST, count), 0).astype(F32)
+    held = (key >= start) & (key < start + rows)
+    chosen = jnp.where(held & (rank == turn), local.astype(F32) + 1.0, 0.0)
+    found = [jnp.sum(chosen[n : n + 1]).astype(jnp.int32) - 1 for n in range(MOST)]
+
+    def copies(n):
+        row = jnp.maximum(found[n], 0)
         block = pl.ds(pl.multiple_of(row // 8 * 8, 8), 8)
         strip = pl.ds(pl.multiple_of(row // 128 * 128, 128), 128)
         return (
-            pltpu.make_async_copy(basis.at[block, :], blocks.at[slot], sem.at[0, slot]),
-            pltpu.make_async_copy(snaps.at[:, strip], strips.at[slot], sem.at[1, slot]),
+            pltpu.make_async_copy(basis.at[block, :], blocks.at[n], sem.at[0, n]),
+            pltpu.make_async_copy(snaps.at[:, strip], strips.at[n], sem.at[1, n]),
         )
 
-    for slot in range(MOST):
-        found[slot] = 0
-        place[slot] = 0
-
-    def look(i, slot):
-        row = wanted[i] - start
-        held = (row >= 0) & (row < rows) & (slot < MOST)
-
-        @pl.when(held)
+    for n in range(MOST):
+
+        @pl.when(found[n] >= 0)
         def _():
-            found[slot] = row
-            place[slot] = i
-            for copy in copies(slot, row):
+            for copy in copies(n):
                 copy.start()
 
-        return slot + held.astype(jnp.int32)
-
-    used = lax.fori_loop(0, count, look, 0, unroll=8)
-    table[...] = jnp.zeros(table.shape, F32)
-    for slot in range(MOST):
-
-        @pl.when(slot < used)
+    for n in range(MOST):
+
+        @pl.when(found[n] >= 0)
         def _():
-            for copy in copies(slot, found[slot]):
+            for copy in copies(n):
                 copy.wait()
 
-    lanes = lax.broadcasted_iota(jnp.int32, (8, 128), 1)
-    for slot in range(MOST):
-        row = found[slot]
-        hit = jnp.where(lanes == row % 128, 1.0, 0.0)
-        shots = lax.dot_general(
-            hit, strips[slot], NT, precision=lax.Precision.HIGHEST, preferred_element_type=F32
-        )
-        staged[slot, :, :half] = blocks[slot, pl.ds(row % 8, 1), :]
-        staged[slot, :, half:] = shots[0:1]
-    for slot in range(MOST):
-
-        @pl.when(slot < used)
-        def _():
-            table[pl.ds(place[slot], 1)] = staged[pl.ds(slot, 1)]
+    lanes = lax.broadcasted_iota(jnp.int32, (shots, 128), 1)
+    sublanes = lax.broadcasted_iota(jnp.int32, (MOST, half), 0)
+    modes = jnp.zeros((MOST, half), F32)
+    columns = jnp.zeros((shots, 128), F32)
+    for n in range(MOST):
+        row = jnp.maximum(found[n], 0)
+        taken = jnp.broadcast_to(blocks[n, pl.ds(row % 8, 1), :], modes.shape)
+        modes = jnp.where((sublanes == n) & (found[n] >= 0), taken, modes)
+        moved = pltpu.roll(strips[n], (n + 128 - row % 128) % 128, 1)
+        columns = jnp.where((lanes == n) & (found[n] >= 0), moved, columns)
+    sends[:, :, :half] = jnp.broadcast_to(modes[None], (deep, MOST, half))
+    sends[:, :, half:] = jnp.broadcast_to(columns.T[None, :MOST], (deep, MOST, shots))
 
 
 def pick(sizes, wanted, basis, snaps):
     half, shots = basis.shape[1], snaps.shape[0]
-    anywhere = pl.BlockSpec(memory_space=pl.ANY)
+    count = wanted.shape[0]
+    outside = pl.BlockSpec(memory_space=pl.ANY)
+    inside = pl.BlockSpec(memory_space=pltpu.VMEM)
     return pl.pallas_call(
         functools.partial(pick_body, sizes),
-        out_shape=jax.ShapeDtypeStruct((wanted.shape[0], 1, half + shots), F32),
-        in_specs=[pl.BlockSpec(memory_space=pltpu.SMEM), anywhere, anywhere],
-        out_specs=pl.BlockSpec(memory_space=pltpu.VMEM),
+        out_shape=(
+            jax.ShapeDtypeStruct((sizes[1] * sizes[2], MOST, half + shots), F32),
+            jax.ShapeDtypeStruct((8, count), F32),
+            jax.ShapeDtypeStruct((1,), jnp.int32),
+        ),
+        in_specs=[inside, outside, outside],
+        out_specs=(inside, inside, pl.BlockSpec(memory_space=pltpu.SMEM)),
         scratch_shapes=[
             pltpu.VMEM((MOST, 8, half), F32),
             pltpu.VMEM((MOST, shots, 128), F32),
-            pltpu.VMEM((MOST, 1, half + shots), F32),
-            pltpu.SMEM((MOST,), jnp.int32),
-            pltpu.SMEM((MOST,), jnp.int32),
             pltpu.SemaphoreType.DMA((2, MOST)),
         ],
-        compiler_params=pltpu.CompilerParams(vmem_limit_bytes=60 * 1024 * 1024),
+        compiler_params=pltpu.CompilerParams(vmem_limit_bytes=PICK_VMEM),
         name="pick",
-    )(wanted, basis, snaps)
-
-
-def share_body(parts, copies):
-    copies[...] = jnp.broadcast_to(jnp.sum(parts[...], axis=0, keepdims=True), copies.shape)
-
-
-def share(parts):
+    )(wanted.reshape(1, count), basis, snaps)
+
+
+def dot_exact(choice, right):
+    total = None
+    for _ in range(3):
+        piece = right.astype(BF16)
+        right = right - piece.astype(F32)
+        part = jnp.dot(choice, piece, preferred_element_type=F32)
+        total = part if total is None else total + part
+    return total
+
+
+def pack_body(gathered, places, sends):
+    half = sends.shape[2]
+    room = sends.shape[1] // 3 * 2
+    width = gathered.shape[2]
+    count = places.shape[1]
+    slots = gathered.shape[0] * gathered.shape[1]
+    here = lax.axis_index(ROWS[0]).astype(F32)
+    place = jnp.where(places[1:2] == here, places[0:1], -1.0)
+    wanted = lax.broadcasted_iota(jnp.int32, (room, count), 0).astype(F32) == place
+    slot = lax.broadcasted_iota(jnp.int32, (slots, count), 0).astype(F32) == places[2:3]
+    ones = lambda hit: jnp.where(hit, 1.0, 0.0).astype(BF16)
+    choice = lax.dot_general(ones(wanted), ones(slot), NT, preferred_element_type=F32)
+    packed = dot_exact(choice.astype(BF16), gathered[...].reshape(slots, width))
+    pairs = [packed[: room // 2, half:], packed[room // 2 :, half:]]
+    packed = jnp.concatenate([packed[:, :half], jnp.concatenate(pairs, axis=1)], axis=0)
+    sends[...] = jnp.broadcast_to(packed[None], sends.shape)
+
+
+def unpack_body(received, places, modes, shots):
+    peers = received.shape[0]
+    half = modes.shape[1]
+    room = received.shape[1] // 3 * 2
+    count = places.shape[1]
+    address = places[1:2] * room + places[0:1]
+    address = jnp.broadcast_to(address, (128, count)).T
+    address = jnp.concatenate([address] * (peers * room // 128), axis=1)
+    column = lax.broadcasted_iota(jnp.int32, address.shape, 1).astype(F32)
+    choice = jnp.where(address == column, 1.0, 0.0).astype(BF16)
+    pairs = received[:, room:, :]
+    tall = jnp.concatenate([pairs[:, :, : half // 2], pairs[:, :, half // 2 :]], axis=1)
+    rows = jnp.concatenate([received[:, :room, :], tall], axis=2)
+    table = dot_exact(choice, rows.reshape(peers * room, half + half // 2))
+    modes[...] = table[:, :half]
+    shots[...] = table[:, half:]
+
+
+def inside_kernel(body, name, out_shape, *args):
     inside = pl.BlockSpec(memory_space=pltpu.VMEM)
     return pl.pallas_call(
-        share_body,
-        out_shape=jax.ShapeDtypeStruct(parts.shape, F32),
-        in_specs=[inside],
-        out_specs=inside,
-        compiler_params=pltpu.CompilerParams(vmem_limit_bytes=8 * 1024 * 1024),
-        name="share",
-    )(parts)
+        body,
+        out_shape=out_shape,
+        in_specs=[inside] * len(args),
+        out_specs=jax.tree.map(lambda _: inside, out_shape),
+        compiler_params=pltpu.CompilerParams(vmem_limit_bytes=16 * 1024 * 1024),
+        name=name,
+    )(*args)
+
+
+def along_planes(planes, half, room, gathered, places):
+    width = gathered.shape[2]
+    count = places.shape[1]
+    shape = jax.ShapeDtypeStruct
+    sends = inside_kernel(pack_body, "pack", shape((planes, room + room // 2, half), F32), gathered, places)
+    received = lax.all_to_all(sends, ROWS[0], 0, 0, tiled=True)
+    out = (shape((count, half), F32), shape((count, width - half), F32))
+    return inside_kernel(unpack_body, "unpack", out, received, places)
 
 
 def root_mean_body(total_rows, squares, out):
@@ -265,11 +334,17 @@
 
 def on_device(sizes, sample_rows, basis, snapshots):
     snaps = snapshots.T
+    half = basis.shape[1]
     other = lax.ppermute(basis, "modes", [(0, 1), (1, 0)])
-    parts = exchange(pick(sizes, sample_rows, basis, snaps))
-    table = exchange(share(parts))
-    swapped = lax.ppermute(table, "modes", [(0, 1), (1, 0)])
-    projector, residual, squares = finish(table, swapped, basis, other, snaps)
+    sends, places, crowded = pick(sizes, sample_rows, basis, snaps)
+    gathered = lax.all_to_all(sends, ROWS[1:], 0, 0, tiled=True)
+    narrow, wide = [
+        functools.partial(along_planes, sizes[0], half, room)
+        for room in (NARROW, sample_rows.shape[0])
+    ]
+    modes, shots = lax.cond(crowded[0] > 0, wide, narrow, gathered, places)
+    swapped = lax.ppermute(modes, "modes", [(0, 1), (1, 0)])
+    projector, residual, squares = finish(modes, swapped, shots, basis, other, snaps)
     total_rows = basis.shape[0] * lax.axis_size(ROWS)
     residual_rms = root_mean(exchange(squares), total_rows)
     return (projector, residual.T, residual_rms.reshape(-1))

time: 106 us -> 86.7 us (0.82)
  blocking collectives: 75.3 us -> 44 us
  waiting for transfers between devices: 1.14 us -> 10.6 us
  starting transfers between devices: 13.9 us -> 19.9 us
  Pallas kernels: 14.3 us -> 10.4 us
    all_to_all x3 -> x1, blocking collectives: 75.3 us -> 22.7 us  [exchange(): return lax.all_to_all(blocks, ROWS, 0, 0, tiled=True)]
    all_to_all x0 -> x1, blocking collectives: none -> 21.3 us  [along_planes(): received = lax.all_to_all(sends, ROWS[0], 0, 0, tiled=True)]
    all_to_all x0 -> x1, waiting for transfers between devices: none -> 9.64 us  [on_device(): gathered = lax.all_to_all(sends, ROWS[1:], 0, 0, tiled=True)]
    all_to_all x0 -> x1, starting transfers between devices: none -> 5.05 us  [on_device(): gathered = lax.all_to_all(sends, ROWS[1:], 0, 0, tiled=True)]
    pallas_call x2 -> x3, Pallas kernels: 6.63 us -> 3.06 us  [the longest x1 2.13 us: pick(): pl.pallas_call(functools.partial(pick_body, sizes), out_shape=(jax.ShapeD...]
  transfers between devices with their start and end apart: 2 -> 3, of which waited for: 1 -> 2; matrix products, arithmetic and copies ran while one was open for 0% -> 0% of each run, Pallas kernels for 6% -> 4%
where the time goes in v2:
time: 86.7 us; the launch traced here: 86.2 us
  blocking collectives  44 us (51%)
  starting transfers between devices  19.9 us (23%)
  waiting for transfers between devices  10.6 us (12%)
  Pallas kernels  10.4 us (12%)
  between operations  1.33 us (2%)
    all_to_all x1, blocking collectives, exchange(): return lax.all_to_all(blocks, ROWS, 0, 0, tiled=True)  22.7 us
    all_to_all x1, blocking collectives, along_planes(): received = lax.all_to_all(sends, ROWS[0], 0, 0, tiled=True)  21.3 us
    all_to_all x1, waiting for transfers between devices, on_device(): gathered = lax.all_to_all(sends, ROWS[1:], 0, 0, tiled=True)  9.64 us
    ppermute x1, starting transfers between devices, on_device(): other = lax.ppermute(basis, 'modes', [(0, 1), (1, 0)])  8.75 us
    pallas_call x1, Pallas kernels, finish(): pl.pallas_call(finish_body, out_shape=(jax.ShapeDtypeStruct((rows, half),...  6.56 us
    ppermute x1, starting transfers between devices, on_device(): swapped = lax.ppermute(modes, 'modes', [(0, 1), (1, 0)])  6.06 us
    all_to_all x1, starting transfers between devices, on_device(): gathered = lax.all_to_all(sends, ROWS[1:], 0, 0, tiled=True)  5.05 us
    pallas_call x1, Pallas kernels, pick(): pl.pallas_call(functools.partial(pick_body, sizes), out_shape=(jax.ShapeD...  2.13 us
  transfers between devices with their start and end apart: 3, of which 2 were waited for; matrix products, arithmetic and copies ran while one was open for 0% of the time, Pallas kernels for 4%

profile of v2, /device:TPU:1, one launch (start us, length us, event | category | flops | bytes accessed | tf_op | source)
XLA Modules:
  0.0 86.2 jit_solution(17173865340663630083)
XLA Ops:
  0.6 8.7 %collective-permute-start.1 = (f32[2048,128]{1,0:T(8,128)}, f32[2048,128]{1,0:T(8,128)S(1)}, u32[]{:S(2)}, u32[]{:S(2)}) collective-permute-start(f32[2048,128]{1,0:T(8,128)} %own.1), channel_id=1, source_target_pairs={{0,1},{1,0},{2,3},{3,2},{4,5},{5,4},{6,7},{7,6},{8,9},{9,8},{10,11... | collective-permute-start | bytes 3145736 | tf_op jit(solution)/shard_map/ppermute | solution.py:338
  9.4 2.1 %pick.1 = (f32[32,8,192]{2,1,0:T(8,128)}, f32[8,256]{1,0:T(8,128)S(1)}, s32[1]{0:T(128)}) custom-call(s32[1,256]{1,0:T(1,128)} %bitcast.7, f32[2048,128]{1,0:T(8,128)} %own.1, f32[64,2048]{1,0:T(8,128)} %bitcast.5), custom_call_target="tpu_custom_call" | custom-call | tf_op jit(solution)/shard_map/pick/pallas_call | solution.py:228
  11.5 5.0 %all-to-all-start.2 = ((f32[32,8,192]{2,1,0:T(8,128)}), f32[32,8,192]{2,1,0:T(8,128)S(1)}, u32[]{:S(2)}, u32[]{:S(2)}) async-start(f32[32,8,192]{2,1,0:T(8,128)} %get-tuple-element.24), calls=%async_computation.2 | async-start | bytes 524288 | tf_op jit(solution)/shard_map/all_to_all | solution.py:340
  17.2 9.6 %all-to-all-done.2 = f32[32,8,192]{2,1,0:T(8,128)S(1)} async-done(((f32[32,8,192]{2,1,0:T(8,128)}), f32[32,8,192]{2,1,0:T(8,128)S(1)}, u32[]{:S(2)}, u32[]{:S(2)}) %all-to-all-start.2) | async-done | bytes 196640 | tf_op jit(solution)/shard_map/all_to_all | solution.py:340
  26.9 0.0 copy-start
  26.9 0.0 copy-start.1
  26.9 22.3 %conditional.1 = ((f32[256,128]{1,0:T(8,128)S(1)}, f32[256,64]{1,0:T(8,128)S(1)})) conditional(s32[]{:T(128)} %bitcast.2, (f32[32,8,192]{2,1,0:T(8,128)S(1)}, f32[8,256]{1,0:T(8,128)S(1)}) %tuple.14, (f32[32,8,192]{2,1,0:T(8,128)S(1)}, f32[8,256]{1,0:T(8,128)S(1)}) %tuple.14), branch_computations={%region_0.0_spmd, %region_1.0_spmd} | conditional | bytes 3145736 | solution.py:345
  26.9 0.5 pack.2
  27.3 21.3 %all_to_all.18.received = f32[8,96,128]{2,1,0:T(8,128)S(1)} all-to-all(f32[8,96,128]{2,1,0:T(8,128)S(1)} %pack.2), channel_id=1, replica_groups=mesh['rows_0'=8,'rows_1'=4,'rows_2'=8,'modes'=2] {'rows_0'}, dimensions={0} | all-to-all | bytes 786432 | tf_op jit(solution)/shard_map/cond/branch_0_fun/all_to_all | solution.py:310
  48.7 0.5 unpack.2
  49.2 6.1 %collective-permute-start = (f32[256,128]{1,0:T(8,128)S(1)}, f32[256,128]{1,0:T(8,128)S(1)}, u32[]{:S(2)}, u32[]{:S(2)}) collective-permute-start(f32[256,128]{1,0:T(8,128)S(1)} %get-tuple-element.26.modes), channel_id=1, source_target_pairs={{0,1},{1,0},{2,3},{3,2},{4,5},{5,4},{6,7},{7,6},{8,9},{9,8},{10,11... | collective-permute-start | bytes 393224 | tf_op jit(solution)/shard_map/ppermute | solution.py:346
  55.2 1.0 %collective-permute-done.swapped = f32[256,128]{1,0:T(8,128)S(1)} collective-permute-done((f32[256,128]{1,0:T(8,128)S(1)}, f32[256,128]{1,0:T(8,128)S(1)}, u32[]{:S(2)}, u32[]{:S(2)}) %collective-permute-start) | collective-permute-done | bytes 131104 | tf_op jit(solution)/shard_map/ppermute | solution.py:346
  56.2 0.0 collective-permute-done.1.other
  56.2 0.0 copy-done
  56.2 0.0 copy-done.1
  56.2 6.6 %finish.1 = (f32[2048,128]{1,0:T(8,128)}, f32[64,2048]{1,0:T(8,128)}, f32[256,1,64]{2,1,0:T(1,128)S(1)}) custom-call(f32[256,128]{1,0:T(8,128)S(1)} %get-tuple-element.26.modes, f32[256,128]{1,0:T(8,128)S(1)} %collective-permute-done.swapped, f32[256,64]{1,0:T(8,128)S(1)} %get-tuple-element.27.shots, f32[2048,128]{1,0:T(8,128)S(1)} %copy-done, ...), custom_call_target="tpu_custom_call" | custom-call | flops 201326592 | bytes 6291456 | tf_op jit(solution)/shard_map/finish/pallas_call | solution.py:133
  62.8 22.7 %all_to_all.20.squares = f32[256,1,64]{2,1,0:T(1,128)S(1)} all-to-all(f32[256,1,64]{2,1,0:T(1,128)S(1)} %get-tuple-element.30), channel_id=1, replica_groups=mesh['rows_0'=8,'rows_1'=4,'rows_2'=8,'modes'=2] {'rows_0','rows_1','row..., dimensions={0} | all-to-all | bytes 131072 | tf_op jit(solution)/shard_map/all_to_all | solution.py:332
  85.5 0.8 root_mean.1
Async XLA Ops:
  0.6 55.6 %collective-permute-start.1 = (f32[2048,128]{1,0:T(8,128)}, f32[2048,128]{1,0:T(8,128)S(1)}, u32[]{:S(2)}, u32[]{:S(2)}) collective-permute-start(f32[2048,128]{1,0:T(8,128)} %own.1), channel_id=1, source_target_pairs={{0,1},{1,0},{2,3},{3,2},{4,5},{5,4},{6,7},{7,6},{8,9},{9,8},{10,11... | collective-permute-start | bytes 3145736 | tf_op jit(solution)/shard_map/ppermute | solution.py:338
  11.5 15.3 %all-to-all-start.2 = ((f32[32,8,192]{2,1,0:T(8,128)}), f32[32,8,192]{2,1,0:T(8,128)S(1)}, u32[]{:S(2)}, u32[]{:S(2)}) async-start(f32[32,8,192]{2,1,0:T(8,128)} %get-tuple-element.24), calls=%async_computation.2 | async-start | bytes 524288 | tf_op jit(solution)/shard_map/all_to_all | solution.py:340
  26.9 29.3 %copy-start = (f32[2048,128]{1,0:T(8,128)S(1)}, f32[2048,128]{1,0:T(8,128)}, u32[]{:S(2)}) copy-start(f32[2048,128]{1,0:T(8,128)} %own.1) | copy-start | bytes 3145732
  26.9 29.3 %copy-start.1 = (f32[2048,64]{0,1:T(8,128)S(1)}, f32[2048,64]{0,1:T(8,128)}, u32[]{:S(2)}) copy-start(f32[2048,64]{0,1:T(8,128)} %param.7) | copy-start | bytes 1572868
  49.2 7.0 %collective-permute-start = (f32[256,128]{1,0:T(8,128)S(1)}, f32[256,128]{1,0:T(8,128)S(1)}, u32[]{:S(2)}, u32[]{:S(2)}) collective-permute-start(f32[256,128]{1,0:T(8,128)S(1)} %get-tuple-element.26.modes), channel_id=1, source_target_pairs={{0,1},{1,0},{2,3},{3,2},{4,5},{5,4},{6,7},{7,6},{8,9},{9,8},{10,11... | collective-permute-start | bytes 393224 | tf_op jit(solution)/shard_map/ppermute | solution.py:346

commit v3 on v2

--- a/solution.py
+++ b/solution.py
@@ -15,6 +15,7 @@
 DOUBLINGS = 5
 REFINES = 3
 TILE = 256
+SETTLED = 2e-5
 MOST = 8
 NARROW = 64
 PICK_VMEM = 60 * 1024 * 1024
@@ -23,14 +24,17 @@
 def dot_once(left, right):
     return jnp.dot(left.astype(BF16), right.astype(BF16), preferred_element_type=F32)
 
+
 def dot_full(left, right):
     return jnp.dot(left, right, precision=lax.Precision.HIGHEST, preferred_element_type=F32)
+
 
 def eliminate(matrix, right):
     order, width = matrix.shape
     lanes = lax.broadcasted_iota(jnp.int32, (order, width), 1)
     places = lax.broadcasted_iota(jnp.int32, (order, 1), 0)
     lane = lax.broadcasted_iota(jnp.int32, (1, width), 1)
+
     def step(k, carry):
         row = matrix[pl.ds(k, 1), :]
         scale = 1.0 / jnp.sum(jnp.where(lane == k, row, 0.0), axis=1, keepdims=True)
@@ -43,78 +47,94 @@
         matrix[pl.ds(k, 1), :] = row
         right[pl.ds(k, 1), :] = answer
         return carry
+
     lax.fori_loop(0, order, step, 0)
 
-def solve(sampled, right, matrix, answer):
-    order = sampled.shape[0]
-    i = lax.broadcasted_iota(jnp.int32, (order, order), 0)
-    j = lax.broadcasted_iota(jnp.int32, (order, order), 1)
-    eye = i == j
+
+def scaled_rows(modes, swapped):
+    mode = lax.axis_index("modes")
+    here, there = modes[...], swapped[...]
+    first = jnp.where(mode == 0, here, there)
+    second = jnp.where(mode == 0, there, here)
+    sampled = jnp.concatenate([first, second], axis=1)
+    eye = diagonal_of(sampled.shape)
     scale = 1.0 / jnp.sum(jnp.where(eye, sampled, 0.0), axis=1, keepdims=True)
-    scaled = jnp.where(eye, 1.0, sampled * scale)
-    right = right * scale
+    return jnp.where(eye, 1.0, sampled * scale), scale
+
+
+def diagonal_of(shape):
+    i = lax.broadcasted_iota(jnp.int32, shape, 0)
+    j = lax.broadcasted_iota(jnp.int32, shape, 1)
+    return i == j
+
+
+def nearly_inverse(scaled):
+    eye = diagonal_of(scaled.shape)
     power = jnp.where(eye, 0.0, -scaled)
     guess = jnp.where(eye, 1.0, power)
     for _ in range(DOUBLINGS):
         low = power.astype(BF16)
         power = jnp.dot(low, low, preferred_element_type=F32)
         guess = guess + dot_once(power, guess)
-    guess = guess.astype(BF16)
+    return guess.astype(BF16)
+
+
+def refine(scaled, guess, right, matrix, answer):
     out = jnp.dot(guess, right.astype(BF16), preferred_element_type=F32)
     for _ in range(REFINES):
-        fix = jnp.dot(guess, (right - dot_full(scaled, out)).astype(BF16), preferred_element_type=F32)
+        left = (right - dot_full(scaled, out)).astype(BF16)
+        fix = jnp.dot(guess, left, preferred_element_type=F32)
         out = out + fix
     answer[...] = out
     size = jnp.max(jnp.abs(out), axis=0, keepdims=True)
     change = jnp.max(jnp.abs(fix), axis=0, keepdims=True)
-    settled = jnp.min(jnp.where(change <= 1e-4 * size, 1.0, 0.0))
-    @pl.when(settled < 0.5)
+    settled = jnp.min(jnp.where(change <= SETTLED * size, 1.0, 0.0))
+
+    @pl.when(jnp.logical_not(settled > 0.5))
     def _():
         matrix[...] = scaled
         answer[...] = right
         eliminate(matrix, answer)
 
-def finish_body(modes, swapped, shots, own, other, snaps, projector, residual, squares,
-                modes_v, snaps_v, projector_v, residual_v, matrix, answer, sem_in, sem_out):
-    rows, half = own.shape
+
+def load_modes(own, other, modes_v, sem):
+    half = own.shape[1]
     mode = lax.axis_index("modes")
     mine = pl.ds(pl.multiple_of(mode * half, half), half)
     theirs = pl.ds(pl.multiple_of((1 - mode) * half, half), half)
     loads = [
-        pltpu.make_async_copy(own, modes_v.at[:, mine], sem_in.at[0]),
-        pltpu.make_async_copy(other, modes_v.at[:, theirs], sem_in.at[1]),
-        pltpu.make_async_copy(snaps, snaps_v, sem_in.at[2]),
+        pltpu.make_async_copy(own, modes_v.at[:, mine], sem.at[0]),
+        pltpu.make_async_copy(other, modes_v.at[:, theirs], sem.at[1]),
     ]
     for load in loads:
         load.start()
-    here, there = modes[...], swapped[...]
-    first = jnp.where(mode == 0, here, there)
-    second = jnp.where(mode == 0, there, here)
-    sampled = jnp.concatenate([first, second], axis=1)
-    picked = shots[...]
-    order = sampled.shape[0]
-    i = lax.broadcasted_iota(jnp.int32, (order, half), 0)
-    j = lax.broadcasted_iota(jnp.int32, (order, half), 1)
-    columns = jnp.where(i == j + mode * half, 1.0, 0.0)
-    solve(sampled, jnp.concatenate([columns, picked], axis=1), matrix, answer)
+    return loads
+
+
+def fit_body(
+    modes, swapped, shots, own, other, snaps, residual, squares, guess_out,
+    modes_v, snaps_v, residual_v, matrix, answer, sem_in, sem_out,
+):
+    loads = load_modes(own, other, modes_v, sem_in)
+    loads.append(pltpu.make_async_copy(snaps, snaps_v, sem_in.at[2]))
+    loads[-1].start()
+    scaled, scale = scaled_rows(modes, swapped)
+    guess = nearly_inverse(scaled)
+    guess_out[...] = guess
+    refine(scaled, guess, shots[...] * scale, matrix, answer)
+    coeffs = answer[...]
     for load in loads:
         load.wait()
-    solved = answer[...]
     total = jnp.zeros((snaps.shape[0], TILE), F32)
     stores = []
-    for at in range(0, rows, TILE):
+    for n, at in enumerate(range(0, own.shape[0], TILE)):
         tile = pl.ds(at, TILE)
-        product = dot_full(modes_v[tile, :], solved)
-        projector_v[tile, :] = product[:, :half]
-        left = snaps_v[:, tile] - product[:, half:].T
+        left = snaps_v[:, tile] - dot_full(modes_v[tile, :], coeffs).T
         residual_v[:, tile] = left
         total = total + left * left
-        n = at // TILE
-        stores += [
-            pltpu.make_async_copy(projector_v.at[tile, :], projector.at[tile, :], sem_out.at[0, n]),
-            pltpu.make_async_copy(residual_v.at[:, tile], residual.at[:, tile], sem_out.at[1, n]),
-        ]
-        stores[-2].start()
+        stores.append(
+            pltpu.make_async_copy(residual_v.at[:, tile], residual.at[:, tile], sem_out.at[n])
+        )
         stores[-1].start()
     sums = lax.dot_general(
         jnp.ones((8, TILE), F32), total, NT,
@@ -124,28 +144,89 @@
     for store in stores:
         store.wait()
 
-def finish(modes, swapped, shots, own, other, snaps):
+
+def fit(modes, swapped, shots, own, other, snaps):
     rows, half = own.shape
     depth = snaps.shape[0]
     order = modes.shape[0]
-    anyspace = pl.BlockSpec(memory_space=pl.ANY)
-    vm = pl.BlockSpec(memory_space=pltpu.VMEM)
+    anywhere = pl.BlockSpec(memory_space=pl.ANY)
+    inside = pl.BlockSpec(memory_space=pltpu.VMEM)
     return pl.pallas_call(
-        finish_body,
-        out_shape=(jax.ShapeDtypeStruct((rows, half), F32), jax.ShapeDtypeStruct((depth, rows), F32),
-                   jax.ShapeDtypeStruct((order, 1, depth), F32)),
-        in_specs=[vm, vm, vm, anyspace, anyspace, anyspace],
-        out_specs=(anyspace, anyspace, vm),
+        fit_body,
+        out_shape=(
+            jax.ShapeDtypeStruct((depth, rows), F32),
+            jax.ShapeDtypeStruct((order, 1, depth), F32),
+            jax.ShapeDtypeStruct((order, order), BF16),
+        ),
+        in_specs=[inside, inside, inside, anywhere, anywhere, anywhere],
+        out_specs=(anywhere, inside, inside),
         scratch_shapes=[
-            pltpu.VMEM((rows, 2 * half), F32), pltpu.VMEM((depth, rows), F32),
-            pltpu.VMEM((rows, half), F32), pltpu.VMEM((depth, rows), F32),
-            pltpu.VMEM((order, order), F32), pltpu.VMEM((order, half + depth), F32),
-            pltpu.SemaphoreType.DMA((3,)), pltpu.SemaphoreType.DMA((2, rows // TILE)),
+            pltpu.VMEM((rows, 2 * half), F32),
+            pltpu.VMEM((depth, rows), F32),
+            pltpu.VMEM((depth, rows), F32),
+            pltpu.VMEM((order, order), F32),
+            pltpu.VMEM((order, depth), F32),
+            pltpu.SemaphoreType.DMA((3,)),
+            pltpu.SemaphoreType.DMA((rows // TILE,)),
         ],
-        compiler_params=pltpu.CompilerParams(vmem_limit_bytes=32 * 1024 * 1024),
-        cost_estimate=pl.CostEstimate(flops=2*rows*256*192, bytes_accessed=6*1024*1024, transcendentals=0),
-        name="finish",
+        compiler_params=pltpu.CompilerParams(vmem_limit_bytes=24 * 1024 * 1024),
+        cost_estimate=pl.CostEstimate(
+            flops=12 * rows * order * depth, bytes_accessed=16 * rows * half, transcendentals=0
+        ),
+        name="fit",
     )(modes, swapped, shots, own, other, snaps)
+
+
+def project_body(
+    modes, swapped, guess, own, other, projector,
+    modes_v, projector_v, matrix, answer, sem_in, sem_out,
+):
+    half = own.shape[1]
+    loads = load_modes(own, other, modes_v, sem_in)
+    scaled, scale = scaled_rows(modes, swapped)
+    i = lax.broadcasted_iota(jnp.int32, (scaled.shape[0], half), 0)
+    j = lax.broadcasted_iota(jnp.int32, (scaled.shape[0], half), 1)
+    columns = jnp.where(i == j + lax.axis_index("modes") * half, scale, 0.0)
+    refine(scaled, guess[...], columns, matrix, answer)
+    inverse = answer[...]
+    for load in loads:
+        load.wait()
+    stores = []
+    for n, at in enumerate(range(0, own.shape[0], TILE)):
+        tile = pl.ds(at, TILE)
+        projector_v[tile, :] = dot_full(modes_v[tile, :], inverse)
+        stores.append(
+            pltpu.make_async_copy(projector_v.at[tile, :], projector.at[tile, :], sem_out.at[n])
+        )
+        stores[-1].start()
+    for store in stores:
+        store.wait()
+
+
+def project(modes, swapped, guess, own, other):
+    rows, half = own.shape
+    order = modes.shape[0]
+    anywhere = pl.BlockSpec(memory_space=pl.ANY)
+    inside = pl.BlockSpec(memory_space=pltpu.VMEM)
+    return pl.pallas_call(
+        project_body,
+        out_shape=jax.ShapeDtypeStruct((rows, half), F32),
+        in_specs=[inside, inside, inside, anywhere, anywhere],
+        out_specs=anywhere,
+        scratch_shapes=[
+            pltpu.VMEM((rows, 2 * half), F32),
+            pltpu.VMEM((rows, half), F32),
+            pltpu.VMEM((order, order), F32),
+            pltpu.VMEM((order, half), F32),
+            pltpu.SemaphoreType.DMA((2,)),
+            pltpu.SemaphoreType.DMA((rows // TILE,)),
+        ],
+        compiler_params=pltpu.CompilerParams(vmem_limit_bytes=24 * 1024 * 1024),
+        cost_estimate=pl.CostEstimate(
+            flops=12 * rows * order * half, bytes_accessed=12 * rows * half, transcendentals=0
+        ),
+        name="project",
+    )(modes, swapped, guess, own, other)
 
 
 def pick_body(sizes, wanted, basis, snaps, sends, places, crowded, blocks, strips, sem):
@@ -290,7 +371,7 @@
     shots[...] = table[:, half:]
 
 
-def inside_kernel(body, name, out_shape, *args):
+def inside_kernel(body, out_shape, *args):
     inside = pl.BlockSpec(memory_space=pltpu.VMEM)
     return pl.pallas_call(
         body,
@@ -298,7 +379,6 @@
         in_specs=[inside] * len(args),
         out_specs=jax.tree.map(lambda _: inside, out_shape),
         compiler_params=pltpu.CompilerParams(vmem_limit_bytes=16 * 1024 * 1024),
-        name=name,
     )(*args)
 
 
@@ -306,10 +386,10 @@
     width = gathered.shape[2]
     count = places.shape[1]
     shape = jax.ShapeDtypeStruct
-    sends = inside_kernel(pack_body, "pack", shape((planes, room + room // 2, half), F32), gathered, places)
+    sends = inside_kernel(pack_body, shape((planes, room + room // 2, half), F32), gathered, places)
     received = lax.all_to_all(sends, ROWS[0], 0, 0, tiled=True)
     out = (shape((count, half), F32), shape((count, width - half), F32))
-    return inside_kernel(unpack_body, "unpack", out, received, places)
+    return inside_kernel(unpack_body, out, received, places)
 
 
 def root_mean_body(total_rows, squares, out):
@@ -335,18 +415,20 @@
 def on_device(sizes, sample_rows, basis, snapshots):
     snaps = snapshots.T
     half = basis.shape[1]
-    other = lax.ppermute(basis, "modes", [(0, 1), (1, 0)])
     sends, places, crowded = pick(sizes, sample_rows, basis, snaps)
     gathered = lax.all_to_all(sends, ROWS[1:], 0, 0, tiled=True)
+    other = lax.ppermute(basis, "modes", [(0, 1), (1, 0)])
     narrow, wide = [
         functools.partial(along_planes, sizes[0], half, room)
         for room in (NARROW, sample_rows.shape[0])
     ]
     modes, shots = lax.cond(crowded[0] > 0, wide, narrow, gathered, places)
     swapped = lax.ppermute(modes, "modes", [(0, 1), (1, 0)])
-    projector, residual, squares = finish(modes, swapped, shots, basis, other, snaps)
+    residual, squares, guess = fit(modes, swapped, shots, basis, other, snaps)
+    squares = exchange(squares)
+    projector = project(modes, swapped, guess, basis, other)
     total_rows = basis.shape[0] * lax.axis_size(ROWS)
-    residual_rms = root_mean(exchange(squares), total_rows)
+    residual_rms = root_mean(squares, total_rows)
     return (projector, residual.T, residual_rms.reshape(-1))
 
 

time: 86.7 us -> 87.5 us (level)
  blocking collectives: 44 us -> 21.4 us
  starting transfers between devices: 19.9 us -> 29.9 us
  waiting for transfers between devices: 10.6 us -> 17.5 us
  Pallas kernels: 10.4 us -> 16.9 us
    all_to_all x1 -> x0, blocking collectives: 22.7 us -> none  [exchange(): return lax.all_to_all(blocks, ROWS, 0, 0, tiled=True)]
    all_to_all x0 -> x1, starting transfers between devices: none -> 10.8 us  [exchange(): return lax.all_to_all(blocks, ROWS, 0, 0, tiled=True)]
    all_to_all x0 -> x1, waiting for transfers between devices: none -> 6.89 us  [exchange(): return lax.all_to_all(blocks, ROWS, 0, 0, tiled=True)]
    pallas_call x1 -> x2, Pallas kernels: 6.56 us -> 12.3 us  [the longest x1 7.06 us: fit(): pl.pallas_call(fit_body, out_shape=(jax.ShapeDtypeStruct((depth, rows), F...]
  transfers between devices with their start and end apart: 3 -> 4, of which waited for: 2 -> 3; matrix products, arithmetic and copies ran while one was open for 0% -> 0% of each run, Pallas kernels for 4% -> 10%
where the time goes in v3:
time: 87.5 us; the launch traced here: 87.1 us
  starting transfers between devices  29.9 us (34%)
  blocking collectives  21.4 us (24%)
  waiting for transfers between devices  17.5 us (20%)
  Pallas kernels  16.9 us (19%)
  between operations  1.35 us (2%)
    all_to_all x1, blocking collectives, along_planes(): received = lax.all_to_all(sends, ROWS[0], 0, 0, tiled=True)  21.4 us
    all_to_all x1, starting transfers between devices, exchange(): return lax.all_to_all(blocks, ROWS, 0, 0, tiled=True)  10.8 us
    all_to_all x1, waiting for transfers between devices, on_device(): gathered = lax.all_to_all(sends, ROWS[1:], 0, 0, tiled=True)  9.64 us
    ppermute x1, starting transfers between devices, on_device(): other = lax.ppermute(basis, 'modes', [(0, 1), (1, 0)])  8.75 us
    pallas_call x1, Pallas kernels, fit(): pl.pallas_call(fit_body, out_shape=(jax.ShapeDtypeStruct((depth, rows), F...  7.06 us
    all_to_all x1, waiting for transfers between devices, exchange(): return lax.all_to_all(blocks, ROWS, 0, 0, tiled=True)  6.89 us
    ppermute x1, starting transfers between devices, on_device(): swapped = lax.ppermute(modes, 'modes', [(0, 1), (1, 0)])  6.06 us
    pallas_call x1, Pallas kernels, project(): pl.pallas_call(project_body, out_shape=jax.ShapeDtypeStruct((rows, half),...  5.24 us
  transfers between devices with their start and end apart: 4, of which 3 were waited for; matrix products, arithmetic and copies ran while one was open for 0% of the time, Pallas kernels for 10%

profile of v3, /device:TPU:1, one launch (start us, length us, event | category | flops | bytes accessed | tf_op | source)
XLA Modules:
  0.0 87.1 jit_solution(5542708769024050759)
XLA Ops:
  0.6 8.7 %collective-permute-start.1 = (f32[2048,128]{1,0:T(8,128)}, f32[2048,128]{1,0:T(8,128)S(1)}, u32[]{:S(2)}, u32[]{:S(2)}) collective-permute-start(f32[2048,128]{1,0:T(8,128)} %own.3), channel_id=1, source_target_pairs={{0,1},{1,0},{2,3},{3,2},{4,5},{5,4},{6,7},{7,6},{8,9},{9,8},{10,11... | collective-permute-start | bytes 3145736 | tf_op jit(solution)/shard_map/ppermute | solution.py:420
  9.4 2.9 %pick.1 = (f32[32,8,192]{2,1,0:T(8,128)}, f32[8,256]{1,0:T(8,128)S(1)}, s32[1]{0:T(128)}) custom-call(s32[1,256]{1,0:T(1,128)} %bitcast.7, f32[2048,128]{1,0:T(8,128)} %own.3, f32[64,2048]{1,0:T(8,128)} %bitcast.5), custom_call_target="tpu_custom_call" | custom-call | tf_op jit(solution)/shard_map/pick/pallas_call | solution.py:309
  12.3 4.3 %all-to-all-start.2 = ((f32[32,8,192]{2,1,0:T(8,128)}), f32[32,8,192]{2,1,0:T(8,128)S(1)}, u32[]{:S(2)}, u32[]{:S(2)}) async-start(f32[32,8,192]{2,1,0:T(8,128)} %get-tuple-element.24), calls=%async_computation.2 | async-start | bytes 524288 | tf_op jit(solution)/shard_map/all_to_all | solution.py:419
  17.3 9.6 %all-to-all-done.2 = f32[32,8,192]{2,1,0:T(8,128)S(1)} async-done(((f32[32,8,192]{2,1,0:T(8,128)}), f32[32,8,192]{2,1,0:T(8,128)S(1)}, u32[]{:S(2)}, u32[]{:S(2)}) %all-to-all-start.2) | async-done | bytes 196640 | tf_op jit(solution)/shard_map/all_to_all | solution.py:419
  26.9 0.0 copy-start
  26.9 0.0 copy-start.1
  26.9 22.3 %conditional.1 = ((f32[256,128]{1,0:T(8,128)S(1)}, f32[256,64]{1,0:T(8,128)S(1)})) conditional(s32[]{:T(128)} %bitcast.2, (f32[32,8,192]{2,1,0:T(8,128)S(1)}, f32[8,256]{1,0:T(8,128)S(1)}) %tuple.14, (f32[32,8,192]{2,1,0:T(8,128)S(1)}, f32[8,256]{1,0:T(8,128)S(1)}) %tuple.14), branch_computations={%region_0.0_spmd, %region_1.0_spmd} | conditional | bytes 3145736 | solution.py:425
  26.9 0.5 branch_0_fun.2
  27.4 21.4 %all_to_all.18.received = f32[8,96,128]{2,1,0:T(8,128)S(1)} all-to-all(f32[8,96,128]{2,1,0:T(8,128)S(1)} %branch_0_fun.2), channel_id=1, replica_groups=mesh['rows_0'=8,'rows_1'=4,'rows_2'=8,'modes'=2] {'rows_0'}, dimensions={0} | all-to-all | bytes 786432 | tf_op jit(solution)/shard_map/cond/branch_0_fun/all_to_all | solution.py:390
  48.7 0.5 branch_0_fun.3
  49.2 6.1 %collective-permute-start = (f32[256,128]{1,0:T(8,128)S(1)}, f32[256,128]{1,0:T(8,128)S(1)}, u32[]{:S(2)}, u32[]{:S(2)}) collective-permute-start(f32[256,128]{1,0:T(8,128)S(1)} %get-tuple-element.26.modes), channel_id=1, source_target_pairs={{0,1},{1,0},{2,3},{3,2},{4,5},{5,4},{6,7},{7,6},{8,9},{9,8},{10,11... | collective-permute-start | bytes 393224 | tf_op jit(solution)/shard_map/ppermute | solution.py:426
  55.3 1.0 %collective-permute-done.swapped = f32[256,128]{1,0:T(8,128)S(1)} collective-permute-done((f32[256,128]{1,0:T(8,128)S(1)}, f32[256,128]{1,0:T(8,128)S(1)}, u32[]{:S(2)}, u32[]{:S(2)}) %collective-permute-start) | collective-permute-done | bytes 131104 | tf_op jit(solution)/shard_map/ppermute | solution.py:426
  56.3 0.0 collective-permute-done.1.other
  56.3 0.0 copy-done
  56.3 0.0 copy-done.1
  56.3 7.1 %fit.1 = (f32[64,2048]{1,0:T(8,128)}, f32[256,1,64]{2,1,0:T(1,128)}, bf16[256,256]{1,0:T(8,128)(2,1)S(1)}) custom-call(f32[256,128]{1,0:T(8,128)S(1)} %get-tuple-element.26.modes, f32[256,128]{1,0:T(8,128)S(1)} %collective-permute-done.swapped, f32[256,64]{1,0:T(8,128)S(1)} %get-tuple-element.27.shots, f32[2048,128]{1,0:T(8,128)S(1)} %copy-done, ...), custom_call_target="tpu_custom_call" | custom-call | flops 402653184 | bytes 4194304 | tf_op jit(solution)/shard_map/fit/pallas_call | solution.py:154
  63.3 10.8 %all-to-all-start.3 = ((f32[256,1,64]{2,1,0:T(1,128)}), f32[256,1,64]{2,1,0:T(1,128)S(1)}, u32[]{:S(2)}, u32[]{:S(2)}) async-start(f32[256,1,64]{2,1,0:T(1,128)} %get-tuple-element.30), calls=%async_computation.3 | async-start | bytes 262144 | tf_op jit(solution)/shard_map/all_to_all | solution.py:412
  74.1 5.2 %project.1 = f32[2048,128]{1,0:T(8,128)} custom-call(f32[256,128]{1,0:T(8,128)S(1)} %get-tuple-element.26.modes, f32[256,128]{1,0:T(8,128)S(1)} %collective-permute-done.swapped, bf16[256,256]{1,0:T(8,128)(2,1)S(1)} %get-tuple-element.28.guess, f32[2048,128]{1,0:T(8,128)S(1)} %copy-done, f32[2048,128]{1,0:T(8,128)S(1)} %collective-permute-done.1.other), custom_call_target="tpu_custom_call" | custom-call | flops 805306368 | bytes 3145728 | tf_op jit(solution)/shard_map/project/pallas_call | solution.py:211
  79.4 6.9 %all-to-all-done.3.squares = f32[256,1,64]{2,1,0:T(1,128)S(1)} async-done(((f32[256,1,64]{2,1,0:T(1,128)}), f32[256,1,64]{2,1,0:T(1,128)S(1)}, u32[]{:S(2)}, u32[]{:S(2)}) %all-to-all-start.3) | async-done | bytes 65568 | tf_op jit(solution)/shard_map/all_to_all | solution.py:412
  86.3 0.8 root_mean.1
Async XLA Ops:
  0.6 55.6 %collective-permute-start.1 = (f32[2048,128]{1,0:T(8,128)}, f32[2048,128]{1,0:T(8,128)S(1)}, u32[]{:S(2)}, u32[]{:S(2)}) collective-permute-start(f32[2048,128]{1,0:T(8,128)} %own.3), channel_id=1, source_target_pairs={{0,1},{1,0},{2,3},{3,2},{4,5},{5,4},{6,7},{7,6},{8,9},{9,8},{10,11... | collective-permute-start | bytes 3145736 | tf_op jit(solution)/shard_map/ppermute | solution.py:420
  12.3 14.6 %all-to-all-start.2 = ((f32[32,8,192]{2,1,0:T(8,128)}), f32[32,8,192]{2,1,0:T(8,128)S(1)}, u32[]{:S(2)}, u32[]{:S(2)}) async-start(f32[32,8,192]{2,1,0:T(8,128)} %get-tuple-element.24), calls=%async_computation.2 | async-start | bytes 524288 | tf_op jit(solution)/shard_map/all_to_all | solution.py:419
  26.9 29.4 %copy-start = (f32[2048,128]{1,0:T(8,128)S(1)}, f32[2048,128]{1,0:T(8,128)}, u32[]{:S(2)}) copy-start(f32[2048,128]{1,0:T(8,128)} %own.3) | copy-start | bytes 3145732
  26.9 29.4 %copy-start.1 = (f32[2048,64]{0,1:T(8,128)S(1)}, f32[2048,64]{0,1:T(8,128)}, u32[]{:S(2)}) copy-start(f32[2048,64]{0,1:T(8,128)} %param.7) | copy-start | bytes 1572868
  49.2 7.0 %collective-permute-start = (f32[256,128]{1,0:T(8,128)S(1)}, f32[256,128]{1,0:T(8,128)S(1)}, u32[]{:S(2)}, u32[]{:S(2)}) collective-permute-start(f32[256,128]{1,0:T(8,128)S(1)} %get-tuple-element.26.modes), channel_id=1, source_target_pairs={{0,1},{1,0},{2,3},{3,2},{4,5},{5,4},{6,7},{7,6},{8,9},{9,8},{10,11... | collective-permute-start | bytes 393224 | tf_op jit(solution)/shard_map/ppermute | solution.py:426
  63.3 22.9 %all-to-all-start.3 = ((f32[256,1,64]{2,1,0:T(1,128)}), f32[256,1,64]{2,1,0:T(1,128)S(1)}, u32[]{:S(2)}, u32[]{:S(2)}) async-start(f32[256,1,64]{2,1,0:T(1,128)} %get-tuple-element.30), calls=%async_computation.3 | async-start | bytes 262144 | tf_op jit(solution)/shard_map/all_to_all | solution.py:412

commit v4 on v3

--- a/solution.py
+++ b/solution.py
@@ -12,10 +12,10 @@
 F32 = jnp.float32
 BF16 = jnp.bfloat16
 NT = (((1,), (1,)), ((), ()))
-DOUBLINGS = 5
-REFINES = 3
+DOUBLINGS = 4
+REFINES = 2
 TILE = 256
-SETTLED = 2e-5
+SHRINK = 1 / 32
 MOST = 8
 NARROW = 64
 PICK_VMEM = 60 * 1024 * 1024
@@ -27,6 +27,10 @@
 
 def dot_full(left, right):
     return jnp.dot(left, right, precision=lax.Precision.HIGHEST, preferred_element_type=F32)
+
+
+def held(array):
+    return pltpu.with_memory_space_constraint(array, pltpu.VMEM)
 
 
 def eliminate(matrix, right):
@@ -51,9 +55,9 @@
     lax.fori_loop(0, order, step, 0)
 
 
-def scaled_rows(modes, swapped):
+def scaled_rows(table, swapped, half):
     mode = lax.axis_index("modes")
-    here, there = modes[...], swapped[...]
+    here, there = table[:, :half], swapped[:, :half]
     first = jnp.where(mode == 0, here, there)
     second = jnp.where(mode == 0, there, here)
     sampled = jnp.concatenate([first, second], axis=1)
@@ -79,154 +83,175 @@
     return guess.astype(BF16)
 
 
-def refine(scaled, guess, right, matrix, answer):
+def shrinks(scaled, guess):
+    product = None
+    rest = scaled
+    for _ in range(3):
+        piece = rest.astype(BF16)
+        rest = rest - piece.astype(F32)
+        part = jnp.dot(guess, piece, preferred_element_type=F32)
+        product = part if product is None else product + part
+    gap = jnp.where(diagonal_of(scaled.shape), 1.0, 0.0) - product
+    gap = jnp.sum(jnp.abs(gap), axis=1, keepdims=True)
+    rounding = jnp.sum(jnp.abs(guess.astype(F32)), axis=1, keepdims=True) * 2.0**-8
+    return jnp.max(gap + rounding) <= SHRINK
+
+
+def refine(scaled, guess, right):
     out = jnp.dot(guess, right.astype(BF16), preferred_element_type=F32)
     for _ in range(REFINES):
         left = (right - dot_full(scaled, out)).astype(BF16)
-        fix = jnp.dot(guess, left, preferred_element_type=F32)
-        out = out + fix
-    answer[...] = out
-    size = jnp.max(jnp.abs(out), axis=0, keepdims=True)
-    change = jnp.max(jnp.abs(fix), axis=0, keepdims=True)
-    settled = jnp.min(jnp.where(change <= SETTLED * size, 1.0, 0.0))
-
-    @pl.when(jnp.logical_not(settled > 0.5))
+        out = out + jnp.dot(guess, left, preferred_element_type=F32)
+    return out
+
+
+def solve(scaled, guess, right, matrix, answer):
+    answer[...] = refine(scaled, guess, right)
+
+    @pl.when(jnp.logical_not(shrinks(scaled, guess)))
     def _():
         matrix[...] = scaled
         answer[...] = right
         eliminate(matrix, answer)
 
 
-def load_modes(own, other, modes_v, sem):
-    half = own.shape[1]
+def pieces_of(values):
+    pieces = []
+    for _ in range(3):
+        pieces.append(values.astype(BF16))
+        values = values - pieces[-1].astype(F32)
+    return pieces
+
+
+def own_first(answer):
+    half = answer.shape[0] // 2
     mode = lax.axis_index("modes")
-    mine = pl.ds(pl.multiple_of(mode * half, half), half)
-    theirs = pl.ds(pl.multiple_of((1 - mode) * half, half), half)
-    loads = [
-        pltpu.make_async_copy(own, modes_v.at[:, mine], sem.at[0]),
-        pltpu.make_async_copy(other, modes_v.at[:, theirs], sem.at[1]),
-    ]
-    for load in loads:
-        load.start()
-    return loads
+    mine = answer[pl.ds(pl.multiple_of(mode * half, half), half), :]
+    theirs = answer[pl.ds(pl.multiple_of((1 - mode) * half, half), half), :]
+    return jnp.concatenate([mine, theirs], axis=0)
 
 
 def fit_body(
-    modes, swapped, shots, own, other, snaps, residual, squares, guess_out,
-    modes_v, snaps_v, residual_v, matrix, answer, sem_in, sem_out,
+    table, swapped, own, other, snaps, residual, squares, system, guess_out,
+    matrix, answer, system_v, sem,
 ):
-    loads = load_modes(own, other, modes_v, sem_in)
-    loads.append(pltpu.make_async_copy(snaps, snaps_v, sem_in.at[2]))
-    loads[-1].start()
-    scaled, scale = scaled_rows(modes, swapped)
+    scaled, scale = scaled_rows(table, swapped, own.shape[1])
+    system_v[...] = jnp.where(diagonal_of(scaled.shape), scale, scaled)
+    keep = pltpu.make_async_copy(system_v, system, sem)
+    keep.start()
     guess = nearly_inverse(scaled)
     guess_out[...] = guess
-    refine(scaled, guess, shots[...] * scale, matrix, answer)
-    coeffs = answer[...]
-    for load in loads:
-        load.wait()
-    total = jnp.zeros((snaps.shape[0], TILE), F32)
-    stores = []
-    for n, at in enumerate(range(0, own.shape[0], TILE)):
+    solve(scaled, guess, table[:, own.shape[1] :] * scale, matrix, answer)
+    coeffs = own_first(answer)
+    depth = coeffs.shape[1]
+    spread = jnp.concatenate(pieces_of(coeffs), axis=1)
+    total = jnp.zeros((depth, TILE), F32)
+    for at in range(0, own.shape[0], TILE):
         tile = pl.ds(at, TILE)
-        left = snaps_v[:, tile] - dot_full(modes_v[tile, :], coeffs).T
-        residual_v[:, tile] = left
+        rows = jnp.concatenate([own[tile, :], other[tile, :]], axis=1)
+        product = None
+        for piece in pieces_of(rows):
+            part = jnp.dot(piece, spread, preferred_element_type=F32)
+            product = part if product is None else product + part
+        low = product[:, 2 * depth :]
+        folded = product[:, : 2 * depth] + jnp.concatenate([low, jnp.zeros_like(low)], axis=1)
+        folded = folded.T
+        left = snaps[:, tile] - (folded[:depth] + folded[depth:])
+        residual[:, tile] = left
         total = total + left * left
-        stores.append(
-            pltpu.make_async_copy(residual_v.at[:, tile], residual.at[:, tile], sem_out.at[n])
-        )
-        stores[-1].start()
     sums = lax.dot_general(
         jnp.ones((8, TILE), F32), total, NT,
         precision=lax.Precision.HIGHEST, preferred_element_type=F32,
     )
     squares[...] = jnp.broadcast_to(sums[0:1][None], squares.shape)
-    for store in stores:
-        store.wait()
-
-
-def fit(modes, swapped, shots, own, other, snaps):
+    keep.wait()
+
+
+def fit(table, swapped, own, other, snaps):
     rows, half = own.shape
     depth = snaps.shape[0]
-    order = modes.shape[0]
-    anywhere = pl.BlockSpec(memory_space=pl.ANY)
+    order = table.shape[0]
     inside = pl.BlockSpec(memory_space=pltpu.VMEM)
     return pl.pallas_call(
         fit_body,
         out_shape=(
             jax.ShapeDtypeStruct((depth, rows), F32),
-            jax.ShapeDtypeStruct((order, 1, depth), F32),
+            pltpu.HBM((order, 1, depth), F32),
+            pltpu.HBM((order, order), F32),
             jax.ShapeDtypeStruct((order, order), BF16),
         ),
-        in_specs=[inside, inside, inside, anywhere, anywhere, anywhere],
-        out_specs=(anywhere, inside, inside),
+        in_specs=[inside] * 5,
+        out_specs=(inside, inside, pl.BlockSpec(memory_space=pl.ANY), inside),
         scratch_shapes=[
-            pltpu.VMEM((rows, 2 * half), F32),
-            pltpu.VMEM((depth, rows), F32),
-            pltpu.VMEM((depth, rows), F32),
             pltpu.VMEM((order, order), F32),
             pltpu.VMEM((order, depth), F32),
-            pltpu.SemaphoreType.DMA((3,)),
-            pltpu.SemaphoreType.DMA((rows // TILE,)),
+            pltpu.VMEM((order, order), F32),
+            pltpu.SemaphoreType.DMA,
         ],
-        compiler_params=pltpu.CompilerParams(vmem_limit_bytes=24 * 1024 * 1024),
+        compiler_params=pltpu.CompilerParams(vmem_limit_bytes=16 * 1024 * 1024),
         cost_estimate=pl.CostEstimate(
             flops=12 * rows * order * depth, bytes_accessed=16 * rows * half, transcendentals=0
         ),
         name="fit",
-    )(modes, swapped, shots, own, other, snaps)
+    )(held(table), swapped, own, other, snaps)
 
 
 def project_body(
-    modes, swapped, guess, own, other, projector,
-    modes_v, projector_v, matrix, answer, sem_in, sem_out,
+    system, guess, own, other, residual, projector, residual_out,
+    projector_v, matrix, answer, sem_residual, sem_out,
 ):
     half = own.shape[1]
-    loads = load_modes(own, other, modes_v, sem_in)
-    scaled, scale = scaled_rows(modes, swapped)
+    keep = pltpu.make_async_copy(residual, residual_out, sem_residual)
+    keep.start()
+    scaled = system[...]
+    eye = diagonal_of(scaled.shape)
+    scale = jnp.sum(jnp.where(eye, scaled, 0.0), axis=1, keepdims=True)
+    scaled = jnp.where(eye, 1.0, scaled)
     i = lax.broadcasted_iota(jnp.int32, (scaled.shape[0], half), 0)
     j = lax.broadcasted_iota(jnp.int32, (scaled.shape[0], half), 1)
     columns = jnp.where(i == j + lax.axis_index("modes") * half, scale, 0.0)
-    refine(scaled, guess[...], columns, matrix, answer)
-    inverse = answer[...]
-    for load in loads:
-        load.wait()
+    solve(scaled, guess[...], columns, matrix, answer)
+    inverse = own_first(answer)
     stores = []
     for n, at in enumerate(range(0, own.shape[0], TILE)):
         tile = pl.ds(at, TILE)
-        projector_v[tile, :] = dot_full(modes_v[tile, :], inverse)
+        rows = jnp.concatenate([own[tile, :], other[tile, :]], axis=1)
+        projector_v[tile, :] = dot_full(rows, inverse)
         stores.append(
             pltpu.make_async_copy(projector_v.at[tile, :], projector.at[tile, :], sem_out.at[n])
         )
         stores[-1].start()
+    keep.wait()
     for store in stores:
         store.wait()
 
 
-def project(modes, swapped, guess, own, other):
+def project(system, guess, own, other, residual):
     rows, half = own.shape
-    order = modes.shape[0]
+    order = system.shape[0]
     anywhere = pl.BlockSpec(memory_space=pl.ANY)
     inside = pl.BlockSpec(memory_space=pltpu.VMEM)
     return pl.pallas_call(
         project_body,
-        out_shape=jax.ShapeDtypeStruct((rows, half), F32),
-        in_specs=[inside, inside, inside, anywhere, anywhere],
-        out_specs=anywhere,
+        out_shape=(
+            jax.ShapeDtypeStruct((rows, half), F32),
+            jax.ShapeDtypeStruct(residual.shape, F32),
+        ),
+        in_specs=[inside] * 5,
+        out_specs=(anywhere, anywhere),
         scratch_shapes=[
-            pltpu.VMEM((rows, 2 * half), F32),
             pltpu.VMEM((rows, half), F32),
             pltpu.VMEM((order, order), F32),
             pltpu.VMEM((order, half), F32),
-            pltpu.SemaphoreType.DMA((2,)),
+            pltpu.SemaphoreType.DMA,
             pltpu.SemaphoreType.DMA((rows // TILE,)),
         ],
-        compiler_params=pltpu.CompilerParams(vmem_limit_bytes=24 * 1024 * 1024),
+        compiler_params=pltpu.CompilerParams(vmem_limit_bytes=16 * 1024 * 1024),
         cost_estimate=pl.CostEstimate(
             flops=12 * rows * order * half, bytes_accessed=12 * rows * half, transcendentals=0
         ),
         name="project",
-    )(modes, swapped, guess, own, other)
+    )(system, guess, own, other, residual)
 
 
 def pick_body(sizes, wanted, basis, snaps, sends, places, crowded, blocks, strips, sem):
@@ -353,9 +378,8 @@
     sends[...] = jnp.broadcast_to(packed[None], sends.shape)
 
 
-def unpack_body(received, places, modes, shots):
-    peers = received.shape[0]
-    half = modes.shape[1]
+def unpack_body(received, places, table):
+    peers, _, half = received.shape
     room = received.shape[1] // 3 * 2
     count = places.shape[1]
     address = places[1:2] * room + places[0:1]
@@ -366,9 +390,7 @@
     pairs = received[:, room:, :]
     tall = jnp.concatenate([pairs[:, :, : half // 2], pairs[:, :, half // 2 :]], axis=1)
     rows = jnp.concatenate([received[:, :room, :], tall], axis=2)
-    table = dot_exact(choice, rows.reshape(peers * room, half + half // 2))
-    modes[...] = table[:, :half]
-    shots[...] = table[:, half:]
+    table[...] = dot_exact(choice, rows.reshape(peers * room, half + half // 2))
 
 
 def inside_kernel(body, out_shape, *args):
@@ -388,8 +410,7 @@
     shape = jax.ShapeDtypeStruct
     sends = inside_kernel(pack_body, shape((planes, room + room // 2, half), F32), gathered, places)
     received = lax.all_to_all(sends, ROWS[0], 0, 0, tiled=True)
-    out = (shape((count, half), F32), shape((count, width - half), F32))
-    return inside_kernel(unpack_body, out, received, places)
+    return inside_kernel(unpack_body, shape((count, width), F32), received, places)
 
 
 def root_mean_body(total_rows, squares, out):
@@ -422,11 +443,11 @@
         functools.partial(along_planes, sizes[0], half, room)
         for room in (NARROW, sample_rows.shape[0])
     ]
-    modes, shots = lax.cond(crowded[0] > 0, wide, narrow, gathered, places)
-    swapped = lax.ppermute(modes, "modes", [(0, 1), (1, 0)])
-    residual, squares, guess = fit(modes, swapped, shots, basis, other, snaps)
+    table = lax.cond(crowded[0] > 0, wide, narrow, gathered, places)
+    swapped = lax.ppermute(table, "modes", [(0, 1), (1, 0)])
+    residual, squares, system, guess = fit(table, swapped, basis, other, snaps)
     squares = exchange(squares)
-    projector = project(modes, swapped, guess, basis, other)
+    projector, residual = project(system, guess, basis, other, residual)
     total_rows = basis.shape[0] * lax.axis_size(ROWS)
     residual_rms = root_mean(squares, total_rows)
     return (projector, residual.T, residual_rms.reshape(-1))

time: 87.5 us -> 85.6 us (0.978)
  Pallas kernels: 16.9 us -> 14.2 us
  local copies, waits for them, and re-layouts: 0.01 us -> 0.95 us
    pallas_call x1, Pallas kernels: 7.06 us -> 5.02 us  [fit(): pl.pallas_call(fit_body, out_shape=(jax.ShapeDtypeStruct((depth, rows), F...]
    unnamed x4 -> x6, local copies, waits for them, and re-layouts: 0.01 us -> 0.95 us
where the time goes in v4:
time: 85.6 us; the launch traced here: 85.2 us
  starting transfers between devices  29.8 us (35%)
  blocking collectives  21.4 us (25%)
  waiting for transfers between devices  17.5 us (20%)
  Pallas kernels  14.2 us (17%)
  between operations  1.35 us (2%)
  local copies, waits for them, and re-layouts  0.95 us (1%)
    all_to_all x1, blocking collectives, along_planes(): received = lax.all_to_all(sends, ROWS[0], 0, 0, tiled=True)  21.4 us
    all_to_all x1, starting transfers between devices, exchange(): return lax.all_to_all(blocks, ROWS, 0, 0, tiled=True)  10.6 us
    all_to_all x1, waiting for transfers between devices, on_device(): gathered = lax.all_to_all(sends, ROWS[1:], 0, 0, tiled=True)  9.64 us
    ppermute x1, starting transfers between devices, on_device(): other = lax.ppermute(basis, 'modes', [(0, 1), (1, 0)])  8.75 us
    all_to_all x1, waiting for transfers between devices, exchange(): return lax.all_to_all(blocks, ROWS, 0, 0, tiled=True)  6.75 us
    ppermute x1, starting transfers between devices, on_device(): swapped = lax.ppermute(table, 'modes', [(0, 1), (1, 0)])  6.06 us
    pallas_call x1, Pallas kernels, fit(): pl.pallas_call(fit_body, out_shape=(jax.ShapeDtypeStruct((depth, rows), F...  5.02 us
    pallas_call x1, Pallas kernels, project(): pl.pallas_call(project_body, out_shape=(jax.ShapeDtypeStruct((rows, half)...  4.58 us
  transfers between devices with their start and end apart: 4, of which 3 were waited for; matrix products, arithmetic and copies ran while one was open for 0% of the time, Pallas kernels for 10%

profile of v4, /device:TPU:1, one launch (start us, length us, event | category | flops | bytes accessed | tf_op | source)
XLA Modules:
  0.0 85.2 jit_solution(1409763034695977509)
XLA Ops:
  0.6 8.7 %collective-permute-start.1 = (f32[2048,128]{1,0:T(8,128)}, f32[2048,128]{1,0:T(8,128)S(1)}, u32[]{:S(2)}, u32[]{:S(2)}) collective-permute-start(f32[2048,128]{1,0:T(8,128)} %own.3), channel_id=1, source_target_pairs={{0,1},{1,0},{2,3},{3,2},{4,5},{5,4},{6,7},{7,6},{8,9},{9,8},{10,11... | collective-permute-start | bytes 3145736 | tf_op jit(solution)/shard_map/ppermute | solution.py:441
  9.4 2.9 %pick.1 = (f32[32,8,192]{2,1,0:T(8,128)}, f32[8,256]{1,0:T(8,128)S(1)}, s32[1]{0:T(128)}) custom-call(s32[1,256]{1,0:T(1,128)} %bitcast.7, f32[2048,128]{1,0:T(8,128)} %own.3, f32[64,2048]{1,0:T(8,128)} %bitcast.5), custom_call_target="tpu_custom_call" | custom-call | tf_op jit(solution)/shard_map/pick/pallas_call | solution.py:334
  12.3 4.3 %all-to-all-start.2 = ((f32[32,8,192]{2,1,0:T(8,128)}), f32[32,8,192]{2,1,0:T(8,128)S(1)}, u32[]{:S(2)}, u32[]{:S(2)}) async-start(f32[32,8,192]{2,1,0:T(8,128)} %get-tuple-element.28), calls=%async_computation.2 | async-start | bytes 524288 | tf_op jit(solution)/shard_map/all_to_all | solution.py:440
  17.3 9.6 %all-to-all-done.2 = f32[32,8,192]{2,1,0:T(8,128)S(1)} async-done(((f32[32,8,192]{2,1,0:T(8,128)}), f32[32,8,192]{2,1,0:T(8,128)S(1)}, u32[]{:S(2)}, u32[]{:S(2)}) %all-to-all-start.2) | async-done | bytes 196640 | tf_op jit(solution)/shard_map/all_to_all | solution.py:440
  26.9 0.0 copy-start
  26.9 0.0 copy-start.1
  26.9 22.3 %conditional.1 = (f32[256,192]{1,0:T(8,128)S(1)}) conditional(s32[]{:T(128)} %bitcast.2, (f32[32,8,192]{2,1,0:T(8,128)S(1)}, f32[8,256]{1,0:T(8,128)S(1)}) %tuple.14, (f32[32,8,192]{2,1,0:T(8,128)S(1)}, f32[8,256]{1,0:T(8,128)S(1)}) %tuple.14), branch_computations={%region_0.0_spmd, %region_1.0_spmd} | conditional | bytes 3145736 | solution.py:446
  26.9 0.5 branch_0_fun.2
  27.4 21.4 %all_to_all.18.received = f32[8,96,128]{2,1,0:T(8,128)S(1)} all-to-all(f32[8,96,128]{2,1,0:T(8,128)S(1)} %branch_0_fun.2), channel_id=1, replica_groups=mesh['rows_0'=8,'rows_1'=4,'rows_2'=8,'modes'=2] {'rows_0'}, dimensions={0} | all-to-all | bytes 786432 | tf_op jit(solution)/shard_map/cond/branch_0_fun/all_to_all | solution.py:412
  48.7 0.5 branch_0_fun.3
  49.2 6.1 %collective-permute-start = (f32[256,192]{1,0:T(8,128)S(1)}, f32[256,192]{1,0:T(8,128)S(1)}, u32[]{:S(2)}, u32[]{:S(2)}) collective-permute-start(f32[256,192]{1,0:T(8,128)S(1)} %get-tuple-element.36.table), channel_id=1, source_target_pairs={{0,1},{1,0},{2,3},{3,2},{4,5},{5,4},{6,7},{7,6},{8,9},{9,8},{10,11... | collective-permute-start | bytes 589832 | tf_op jit(solution)/shard_map/ppermute | solution.py:447
  55.3 1.1 %collective-permute-done.swapped = f32[256,192]{1,0:T(8,128)S(1)} collective-permute-done((f32[256,192]{1,0:T(8,128)S(1)}, f32[256,192]{1,0:T(8,128)S(1)}, u32[]{:S(2)}, u32[]{:S(2)}) %collective-permute-start) | collective-permute-done | bytes 196640 | tf_op jit(solution)/shard_map/ppermute | solution.py:447
  56.4 0.0 collective-permute-done.1.other
  56.4 0.0 copy-done
  56.5 0.0 copy-done.1
  56.5 5.0 %fit.1 = (f32[64,2048]{1,0:T(8,128)S(1)}, f32[256,1,64]{2,1,0:T(1,128)}, f32[256,256]{1,0:T(8,128)}, bf16[256,256]{1,0:T(8,128)(2,1)S(1)}) custom-call(f32[256,192]{1,0:T(8,128)S(1)} %get-tuple-element.36.table, f32[256,192]{1,0:T(8,128)S(1)} %collective-permute-done.swapped, f32[2048,128]{1,0:T(8,128)S(1)} %copy-done, ...), custom_call_target="tpu_custom_call" | custom-call | flops 402653184 | bytes 4194304 | tf_op jit(solution)/shard_map/fit/pallas_call | solution.py:175
  61.5 10.6 %all-to-all-start.3 = ((f32[256,1,64]{2,1,0:T(1,128)}), f32[256,1,64]{2,1,0:T(1,128)S(1)}, u32[]{:S(2)}, u32[]{:S(2)}) async-start(f32[256,1,64]{2,1,0:T(1,128)} %get-tuple-element.35), calls=%async_computation.3 | async-start | bytes 262144 | tf_op jit(solution)/shard_map/all_to_all | solution.py:433
  72.1 0.0 copy-start.2
  72.1 0.9 %copy-done.2 = f32[256,256]{1,0:T(8,128)S(1)} copy-done((f32[256,256]{1,0:T(8,128)S(1)}, f32[256,256]{1,0:T(8,128)}, u32[]{:S(2)}) %copy-start.2) | copy-done | bytes 262168
  73.1 4.6 %project.1 = (f32[2048,128]{1,0:T(8,128)}, f32[64,2048]{1,0:T(8,128)}) custom-call(f32[256,256]{1,0:T(8,128)S(1)} %copy-done.2, bf16[256,256]{1,0:T(8,128)(2,1)S(1)} %get-tuple-element.31.guess, f32[2048,128]{1,0:T(8,128)S(1)} %copy-done, f32[2048,128]{1,0:T(8,128)S(1)} %collective-permute-done.1.other, f32[64,2048]{1,0:T(8,128)S(1)} %get-tuple-element.32.residual), custom_call_target="tpu_custom_call" | custom-call | flops 805306368 | bytes 3145728 | tf_op jit(solution)/shard_map/project/pallas_call | solution.py:234
  77.6 6.7 %all-to-all-done.3.squares = f32[256,1,64]{2,1,0:T(1,128)S(1)} async-done(((f32[256,1,64]{2,1,0:T(1,128)}), f32[256,1,64]{2,1,0:T(1,128)S(1)}, u32[]{:S(2)}, u32[]{:S(2)}) %all-to-all-start.3) | async-done | bytes 65568 | tf_op jit(solution)/shard_map/all_to_all | solution.py:433
  84.4 0.8 root_mean.1
Async XLA Ops:
  0.6 55.8 %collective-permute-start.1 = (f32[2048,128]{1,0:T(8,128)}, f32[2048,128]{1,0:T(8,128)S(1)}, u32[]{:S(2)}, u32[]{:S(2)}) collective-permute-start(f32[2048,128]{1,0:T(8,128)} %own.3), channel_id=1, source_target_pairs={{0,1},{1,0},{2,3},{3,2},{4,5},{5,4},{6,7},{7,6},{8,9},{9,8},{10,11... | collective-permute-start | bytes 3145736 | tf_op jit(solution)/shard_map/ppermute | solution.py:441
  12.3 14.6 %all-to-all-start.2 = ((f32[32,8,192]{2,1,0:T(8,128)}), f32[32,8,192]{2,1,0:T(8,128)S(1)}, u32[]{:S(2)}, u32[]{:S(2)}) async-start(f32[32,8,192]{2,1,0:T(8,128)} %get-tuple-element.28), calls=%async_computation.2 | async-start | bytes 524288 | tf_op jit(solution)/shard_map/all_to_all | solution.py:440
  26.9 29.6 %copy-start = (f32[2048,128]{1,0:T(8,128)S(1)}, f32[2048,128]{1,0:T(8,128)}, u32[]{:S(2)}) copy-start(f32[2048,128]{1,0:T(8,128)} %own.3) | copy-start | bytes 3145732
  26.9 29.6 %copy-start.1 = (f32[2048,64]{0,1:T(8,128)S(1)}, f32[2048,64]{0,1:T(8,128)}, u32[]{:S(2)}) copy-start(f32[2048,64]{0,1:T(8,128)} %param.7) | copy-start | bytes 1572868
  49.2 7.2 %collective-permute-start = (f32[256,192]{1,0:T(8,128)S(1)}, f32[256,192]{1,0:T(8,128)S(1)}, u32[]{:S(2)}, u32[]{:S(2)}) collective-permute-start(f32[256,192]{1,0:T(8,128)S(1)} %get-tuple-element.36.table), channel_id=1, source_target_pairs={{0,1},{1,0},{2,3},{3,2},{4,5},{5,4},{6,7},{7,6},{8,9},{9,8},{10,11... | collective-permute-start | bytes 589832 | tf_op jit(solution)/shard_map/ppermute | solution.py:447
  61.5 22.9 %all-to-all-start.3 = ((f32[256,1,64]{2,1,0:T(1,128)}), f32[256,1,64]{2,1,0:T(1,128)S(1)}, u32[]{:S(2)}, u32[]{:S(2)}) async-start(f32[256,1,64]{2,1,0:T(1,128)} %get-tuple-element.35), calls=%async_computation.3 | async-start | bytes 262144 | tf_op jit(solution)/shard_map/all_to_all | solution.py:433
  72.1 1.0 %copy-start.2 = (f32[256,256]{1,0:T(8,128)S(1)}, f32[256,256]{1,0:T(8,128)}, u32[]{:S(2)}) copy-start(f32[256,256]{1,0:T(8,128)} %get-tuple-element.30.system) | copy-start | bytes 786436

commit v5 on v4

--- a/solution.py
+++ b/solution.py
@@ -55,12 +55,7 @@
     lax.fori_loop(0, order, step, 0)
 
 
-def scaled_rows(table, swapped, half):
-    mode = lax.axis_index("modes")
-    here, there = table[:, :half], swapped[:, :half]
-    first = jnp.where(mode == 0, here, there)
-    second = jnp.where(mode == 0, there, here)
-    sampled = jnp.concatenate([first, second], axis=1)
+def scaled_rows(sampled):
     eye = diagonal_of(sampled.shape)
     scale = 1.0 / jnp.sum(jnp.where(eye, sampled, 0.0), axis=1, keepdims=True)
     return jnp.where(eye, 1.0, sampled * scale), scale
@@ -132,16 +127,16 @@
 
 
 def fit_body(
-    table, swapped, own, other, snaps, residual, squares, system, guess_out,
+    sampled, shots, own, other, snaps, residual, squares, system, guess_out,
     matrix, answer, system_v, sem,
 ):
-    scaled, scale = scaled_rows(table, swapped, own.shape[1])
+    scaled, scale = scaled_rows(sampled[...])
     system_v[...] = jnp.where(diagonal_of(scaled.shape), scale, scaled)
     keep = pltpu.make_async_copy(system_v, system, sem)
     keep.start()
     guess = nearly_inverse(scaled)
     guess_out[...] = guess
-    solve(scaled, guess, table[:, own.shape[1] :] * scale, matrix, answer)
+    solve(scaled, guess, shots[...] * scale, matrix, answer)
     coeffs = own_first(answer)
     depth = coeffs.shape[1]
     spread = jnp.concatenate(pieces_of(coeffs), axis=1)
@@ -167,10 +162,10 @@
     keep.wait()
 
 
-def fit(table, swapped, own, other, snaps):
+def fit(sampled, shots, own, other, snaps):
     rows, half = own.shape
     depth = snaps.shape[0]
-    order = table.shape[0]
+    order = sampled.shape[0]
     inside = pl.BlockSpec(memory_space=pltpu.VMEM)
     return pl.pallas_call(
         fit_body,
@@ -193,7 +188,7 @@
             flops=12 * rows * order * depth, bytes_accessed=16 * rows * half, transcendentals=0
         ),
         name="fit",
-    )(held(table), swapped, own, other, snaps)
+    )(held(sampled), held(shots), own, other, snaps)
 
 
 def project_body(
@@ -278,12 +273,6 @@
         return jnp.sum(jnp.where(same, 1.0, 0.0), axis=0, keepdims=True)
 
     rank = earlier(key - local)
-    place = earlier(plane * deep * rows)
-    slot = (line * MOST).astype(F32) + rank
-    empty = jnp.zeros((8 - 3, count), F32)
-    places[...] = jnp.concatenate([place, plane.astype(F32), slot, empty], axis=0)
-    crowded[0] = (jnp.max(place) >= NARROW).astype(jnp.int32)
-
     turn = lax.broadcasted_iota(jnp.int32, (MOST, count), 0).astype(F32)
     held = (key >= start) & (key < start + rows)
     chosen = jnp.where(held & (rank == turn), local.astype(F32) + 1.0, 0.0)
@@ -304,6 +293,12 @@
         def _():
             for copy in copies(n):
                 copy.start()
+
+    place = earlier(plane * deep * rows)
+    slot = (line * MOST).astype(F32) + rank
+    empty = jnp.zeros((8 - 3, count), F32)
+    places[...] = jnp.concatenate([place, plane.astype(F32), slot, empty], axis=0)
+    crowded[0] = (jnp.max(place) >= NARROW).astype(jnp.int32)
 
     for n in range(MOST):
 
@@ -378,7 +373,7 @@
     sends[...] = jnp.broadcast_to(packed[None], sends.shape)
 
 
-def unpack_body(received, places, table):
+def unpack_body(received, places, modes, shots):
     peers, _, half = received.shape
     room = received.shape[1] // 3 * 2
     count = places.shape[1]
@@ -390,7 +385,9 @@
     pairs = received[:, room:, :]
     tall = jnp.concatenate([pairs[:, :, : half // 2], pairs[:, :, half // 2 :]], axis=1)
     rows = jnp.concatenate([received[:, :room, :], tall], axis=2)
-    table[...] = dot_exact(choice, rows.reshape(peers * room, half + half // 2))
+    table = dot_exact(choice, rows.reshape(peers * room, half + half // 2))
+    modes[...] = table[:, :half]
+    shots[...] = table[:, half:]
 
 
 def inside_kernel(body, out_shape, *args):
@@ -410,7 +407,8 @@
     shape = jax.ShapeDtypeStruct
     sends = inside_kernel(pack_body, shape((planes, room + room // 2, half), F32), gathered, places)
     received = lax.all_to_all(sends, ROWS[0], 0, 0, tiled=True)
-    return inside_kernel(unpack_body, shape((count, width), F32), received, places)
+    out = (shape((count, half), F32), shape((count, width - half), F32))
+    return inside_kernel(unpack_body, out, received, places)
 
 
 def root_mean_body(total_rows, squares, out):
@@ -443,9 +441,9 @@
         functools.partial(along_planes, sizes[0], half, room)
         for room in (NARROW, sample_rows.shape[0])
     ]
-    table = lax.cond(crowded[0] > 0, wide, narrow, gathered, places)
-    swapped = lax.ppermute(table, "modes", [(0, 1), (1, 0)])
-    residual, squares, system, guess = fit(table, swapped, basis, other, snaps)
+    modes, shots = lax.cond(crowded[0] > 0, wide, narrow, gathered, places)
+    sampled = lax.all_gather(modes, "modes", axis=1, tiled=True)
+    residual, squares, system, guess = fit(sampled, shots, basis, other, snaps)
     squares = exchange(squares)
     projector, residual = project(system, guess, basis, other, residual)
     total_rows = basis.shape[0] * lax.axis_size(ROWS)

time: 85.6 us -> 84.2 us (0.984)
  starting transfers between devices: 29.8 us -> 23.7 us
  blocking collectives: 21.4 us -> 27.2 us
  waiting for transfers between devices: 17.5 us -> 16.4 us
    ppermute x1 -> x0, starting transfers between devices: 6.06 us -> none  [on_device(): swapped = lax.ppermute(table, 'modes', [(0, 1), (1, 0)])]
    all_gather x0 -> x1, blocking collectives: none -> 5.78 us  [on_device(): sampled = lax.all_gather(modes, 'modes', axis=1, tiled=True)]
    ppermute x1 -> x0, waiting for transfers between devices: 1.14 us -> none  [on_device(): swapped = lax.ppermute(table, 'modes', [(0, 1), (1, 0)])]
  transfers between devices with their start and end apart: 4 -> 3, of which waited for: 3 -> 2; matrix products, arithmetic and copies ran while one was open for 0% -> 0% of each run, Pallas kernels for 10% -> 10%
where the time goes in v5:
time: 84.2 us; the launch traced here: 83.7 us
  blocking collectives  27.2 us (32%)
  starting transfers between devices  23.7 us (28%)
  waiting for transfers between devices  16.4 us (19%)
  Pallas kernels  14.2 us (17%)
  between operations  1.35 us (2%)
  local copies, waits for them, and re-layouts  0.95 us (1%)
    all_to_all x1, blocking collectives, along_planes(): received = lax.all_to_all(sends, ROWS[0], 0, 0, tiled=True)  21.4 us
    all_to_all x1, starting transfers between devices, exchange(): return lax.all_to_all(blocks, ROWS, 0, 0, tiled=True)  10.6 us
    all_to_all x1, waiting for transfers between devices, on_device(): gathered = lax.all_to_all(sends, ROWS[1:], 0, 0, tiled=True)  9.64 us
    ppermute x1, starting transfers between devices, on_device(): other = lax.ppermute(basis, 'modes', [(0, 1), (1, 0)])  8.75 us
    all_to_all x1, waiting for transfers between devices, exchange(): return lax.all_to_all(blocks, ROWS, 0, 0, tiled=True)  6.76 us
    all_gather x1, blocking collectives, on_device(): sampled = lax.all_gather(modes, 'modes', axis=1, tiled=True)  5.78 us
    pallas_call x1, Pallas kernels, fit(): pl.pallas_call(fit_body, out_shape=(jax.ShapeDtypeStruct((depth, rows), F...  5 us
    pallas_call x1, Pallas kernels, project(): pl.pallas_call(project_body, out_shape=(jax.ShapeDtypeStruct((rows, half)...  4.58 us
  transfers between devices with their start and end apart: 3, of which 2 were waited for; matrix products, arithmetic and copies ran while one was open for 0% of the time, Pallas kernels for 10%

profile of v5, /device:TPU:1, one launch (start us, length us, event | category | flops | bytes accessed | tf_op | source)
XLA Modules:
  0.0 83.7 jit_solution(12155218166313357977)
XLA Ops:
  0.6 8.7 %collective-permute-start = (f32[2048,128]{1,0:T(8,128)}, f32[2048,128]{1,0:T(8,128)S(1)}, u32[]{:S(2)}, u32[]{:S(2)}) collective-permute-start(f32[2048,128]{1,0:T(8,128)} %own.3), channel_id=1, source_target_pairs={{0,1},{1,0},{2,3},{3,2},{4,5},{5,4},{6,7},{7,6},{8,9},{9,8},{10,11... | collective-permute-start | bytes 3145736 | tf_op jit(solution)/shard_map/ppermute | solution.py:439
  9.4 2.9 %pick.1 = (f32[32,8,192]{2,1,0:T(8,128)}, f32[8,256]{1,0:T(8,128)S(1)}, s32[1]{0:T(128)}) custom-call(s32[1,256]{1,0:T(1,128)} %bitcast.7, f32[2048,128]{1,0:T(8,128)} %own.3, f32[64,2048]{1,0:T(8,128)} %bitcast.5), custom_call_target="tpu_custom_call" | custom-call | tf_op jit(solution)/shard_map/pick/pallas_call | solution.py:329
  12.3 4.3 %all-to-all-start.2 = ((f32[32,8,192]{2,1,0:T(8,128)}), f32[32,8,192]{2,1,0:T(8,128)S(1)}, u32[]{:S(2)}, u32[]{:S(2)}) async-start(f32[32,8,192]{2,1,0:T(8,128)} %get-tuple-element.27), calls=%async_computation.2 | async-start | bytes 524288 | tf_op jit(solution)/shard_map/all_to_all | solution.py:438
  17.3 9.6 %all-to-all-done.2 = f32[32,8,192]{2,1,0:T(8,128)S(1)} async-done(((f32[32,8,192]{2,1,0:T(8,128)}), f32[32,8,192]{2,1,0:T(8,128)S(1)}, u32[]{:S(2)}, u32[]{:S(2)}) %all-to-all-start.2) | async-done | bytes 196640 | tf_op jit(solution)/shard_map/all_to_all | solution.py:438
  26.9 0.0 copy-start
  26.9 0.0 copy-start.1
  26.9 22.3 %conditional.1 = ((f32[256,128]{1,0:T(8,128)S(1)}, f32[256,64]{1,0:T(8,128)S(1)})) conditional(s32[]{:T(128)} %bitcast.2, (f32[32,8,192]{2,1,0:T(8,128)S(1)}, f32[8,256]{1,0:T(8,128)S(1)}) %tuple.14, (f32[32,8,192]{2,1,0:T(8,128)S(1)}, f32[8,256]{1,0:T(8,128)S(1)}) %tuple.14), branch_computations={%region_0.0_spmd, %region_1.0_spmd} | conditional | bytes 3145736 | solution.py:444
  26.9 0.5 branch_0_fun.2
  27.4 21.4 %all_to_all.18.received = f32[8,96,128]{2,1,0:T(8,128)S(1)} all-to-all(f32[8,96,128]{2,1,0:T(8,128)S(1)} %branch_0_fun.2), channel_id=1, replica_groups=mesh['rows_0'=8,'rows_1'=4,'rows_2'=8,'modes'=2] {'rows_0'}, dimensions={0} | all-to-all | bytes 786432 | tf_op jit(solution)/shard_map/cond/branch_0_fun/all_to_all | solution.py:409
  48.7 0.5 branch_0_fun.3
  49.2 5.8 %all_gather.3.sampled = f32[256,256]{1,0:T(8,128)S(1)} all-gather(f32[256,128]{1,0:T(8,128)S(1)} %get-tuple-element.29), channel_id=1, replica_groups=mesh['rows_0'=8,'rows_1'=4,'rows_2'=8,'modes'=2] {'modes'}, dimensions={1}, use_global_device_ids=true | all-gather | bytes 393216 | tf_op jit(solution)/shard_map/all_gather | solution.py:445
  55.0 0.0 collective-permute-done.other
  55.0 0.0 copy-done
  55.0 0.0 copy-done.1
  55.0 5.0 %fit.1 = (f32[64,2048]{1,0:T(8,128)S(1)}, f32[256,1,64]{2,1,0:T(1,128)}, f32[256,256]{1,0:T(8,128)}, bf16[256,256]{1,0:T(8,128)(2,1)S(1)}) custom-call(f32[256,256]{1,0:T(8,128)S(1)} %all_gather.3.sampled, f32[256,64]{1,0:T(8,128)S(1)} %get-tuple-element.30.shots, f32[2048,128]{1,0:T(8,128)S(1)} %copy-done, f32[2048,128]{1,0:T(8,128)S(1)} %collective-permute-done.other, ...), custom_call_target="tpu_custom_call" | custom-call | flops 402653184 | bytes 4194304 | tf_op jit(solution)/shard_map/fit/pallas_call | solution.py:170
  60.0 10.6 %all-to-all-start.3 = ((f32[256,1,64]{2,1,0:T(1,128)}), f32[256,1,64]{2,1,0:T(1,128)S(1)}, u32[]{:S(2)}, u32[]{:S(2)}) async-start(f32[256,1,64]{2,1,0:T(1,128)} %get-tuple-element.36), calls=%async_computation.3 | async-start | bytes 262144 | tf_op jit(solution)/shard_map/all_to_all | solution.py:431
  70.6 0.0 copy-start.2
  70.7 0.9 %copy-done.2 = f32[256,256]{1,0:T(8,128)S(1)} copy-done((f32[256,256]{1,0:T(8,128)S(1)}, f32[256,256]{1,0:T(8,128)}, u32[]{:S(2)}) %copy-start.2) | copy-done | bytes 262168
  71.6 4.6 %project.1 = (f32[2048,128]{1,0:T(8,128)}, f32[64,2048]{1,0:T(8,128)}) custom-call(f32[256,256]{1,0:T(8,128)S(1)} %copy-done.2, bf16[256,256]{1,0:T(8,128)(2,1)S(1)} %get-tuple-element.32.guess, f32[2048,128]{1,0:T(8,128)S(1)} %copy-done, f32[2048,128]{1,0:T(8,128)S(1)} %collective-permute-done.other, f32[64,2048]{1,0:T(8,128)S(1)} %get-tuple-element.33.residual), custom_call_target="tpu_custom_call" | custom-call | flops 805306368 | bytes 3145728 | tf_op jit(solution)/shard_map/project/pallas_call | solution.py:229
  76.2 6.8 %all-to-all-done.3.squares = f32[256,1,64]{2,1,0:T(1,128)S(1)} async-done(((f32[256,1,64]{2,1,0:T(1,128)}), f32[256,1,64]{2,1,0:T(1,128)S(1)}, u32[]{:S(2)}, u32[]{:S(2)}) %all-to-all-start.3) | async-done | bytes 65568 | tf_op jit(solution)/shard_map/all_to_all | solution.py:431
  83.0 0.8 root_mean.1
Async XLA Ops:
  0.6 54.4 %collective-permute-start = (f32[2048,128]{1,0:T(8,128)}, f32[2048,128]{1,0:T(8,128)S(1)}, u32[]{:S(2)}, u32[]{:S(2)}) collective-permute-start(f32[2048,128]{1,0:T(8,128)} %own.3), channel_id=1, source_target_pairs={{0,1},{1,0},{2,3},{3,2},{4,5},{5,4},{6,7},{7,6},{8,9},{9,8},{10,11... | collective-permute-start | bytes 3145736 | tf_op jit(solution)/shard_map/ppermute | solution.py:439
  12.3 14.6 %all-to-all-start.2 = ((f32[32,8,192]{2,1,0:T(8,128)}), f32[32,8,192]{2,1,0:T(8,128)S(1)}, u32[]{:S(2)}, u32[]{:S(2)}) async-start(f32[32,8,192]{2,1,0:T(8,128)} %get-tuple-element.27), calls=%async_computation.2 | async-start | bytes 524288 | tf_op jit(solution)/shard_map/all_to_all | solution.py:438
  26.9 28.1 %copy-start = (f32[2048,128]{1,0:T(8,128)S(1)}, f32[2048,128]{1,0:T(8,128)}, u32[]{:S(2)}) copy-start(f32[2048,128]{1,0:T(8,128)} %own.3) | copy-start | bytes 3145732
  26.9 28.1 %copy-start.1 = (f32[2048,64]{0,1:T(8,128)S(1)}, f32[2048,64]{0,1:T(8,128)}, u32[]{:S(2)}) copy-start(f32[2048,64]{0,1:T(8,128)} %param.7) | copy-start | bytes 1572868
  60.0 22.9 %all-to-all-start.3 = ((f32[256,1,64]{2,1,0:T(1,128)}), f32[256,1,64]{2,1,0:T(1,128)S(1)}, u32[]{:S(2)}, u32[]{:S(2)}) async-start(f32[256,1,64]{2,1,0:T(1,128)} %get-tuple-element.36), calls=%async_computation.3 | async-start | bytes 262144 | tf_op jit(solution)/shard_map/all_to_all | solution.py:431
  70.6 1.0 %copy-start.2 = (f32[256,256]{1,0:T(8,128)S(1)}, f32[256,256]{1,0:T(8,128)}, u32[]{:S(2)}) copy-start(f32[256,256]{1,0:T(8,128)} %get-tuple-element.31.system) | copy-start | bytes 786436

commit v6 on v5

--- a/solution.py
+++ b/solution.py
@@ -17,7 +17,7 @@
 TILE = 256
 SHRINK = 1 / 32
 MOST = 8
-NARROW = 64
+ROOMS = (48, 64)
 PICK_VMEM = 60 * 1024 * 1024
 
 
@@ -298,7 +298,8 @@
     slot = (line * MOST).astype(F32) + rank
     empty = jnp.zeros((8 - 3, count), F32)
     places[...] = jnp.concatenate([place, plane.astype(F32), slot, empty], axis=0)
-    crowded[0] = (jnp.max(place) >= NARROW).astype(jnp.int32)
+    most = jnp.max(place)
+    crowded[0] = sum((most >= room).astype(jnp.int32) for room in ROOMS)
 
     for n in range(MOST):
 
@@ -437,11 +438,11 @@
     sends, places, crowded = pick(sizes, sample_rows, basis, snaps)
     gathered = lax.all_to_all(sends, ROWS[1:], 0, 0, tiled=True)
     other = lax.ppermute(basis, "modes", [(0, 1), (1, 0)])
-    narrow, wide = [
+    branches = [
         functools.partial(along_planes, sizes[0], half, room)
-        for room in (NARROW, sample_rows.shape[0])
+        for room in (*ROOMS, sample_rows.shape[0])
     ]
-    modes, shots = lax.cond(crowded[0] > 0, wide, narrow, gathered, places)
+    modes, shots = lax.switch(crowded[0], branches, gathered, places)
     sampled = lax.all_gather(modes, "modes", axis=1, tiled=True)
     residual, squares, system, guess = fit(sampled, shots, basis, other, snaps)
     squares = exchange(squares)

time: 84.2 us -> 84.2 us (level)
  no operation moved by 1% of the time
where the time goes in v6:
time: 84.2 us; the launch traced here: 83.8 us
  blocking collectives  27.2 us (32%)
  starting transfers between devices  23.9 us (28%)
  waiting for transfers between devices  16.2 us (19%)
  Pallas kernels  14.2 us (17%)
  between operations  1.35 us (2%)
  local copies, waits for them, and re-layouts  0.95 us (1%)
    all_to_all x1, blocking collectives, along_planes(): received = lax.all_to_all(sends, ROWS[0], 0, 0, tiled=True)  21.4 us
    all_to_all x1, starting transfers between devices, exchange(): return lax.all_to_all(blocks, ROWS, 0, 0, tiled=True)  10.8 us
    all_to_all x1, waiting for transfers between devices, on_device(): gathered = lax.all_to_all(sends, ROWS[1:], 0, 0, tiled=True)  9.64 us
    ppermute x1, starting transfers between devices, on_device(): other = lax.ppermute(basis, 'modes', [(0, 1), (1, 0)])  8.75 us
    all_to_all x1, waiting for transfers between devices, exchange(): return lax.all_to_all(blocks, ROWS, 0, 0, tiled=True)  6.57 us
    all_gather x1, blocking collectives, on_device(): sampled = lax.all_gather(modes, 'modes', axis=1, tiled=True)  5.78 us
    pallas_call x1, Pallas kernels, fit(): pl.pallas_call(fit_body, out_shape=(jax.ShapeDtypeStruct((depth, rows), F...  5 us
    pallas_call x1, Pallas kernels, project(): pl.pallas_call(project_body, out_shape=(jax.ShapeDtypeStruct((rows, half)...  4.59 us
  transfers between devices with their start and end apart: 3, of which 2 were waited for; matrix products, arithmetic and copies ran while one was open for 0% of the time, Pallas kernels for 10%

profile of v6, /device:TPU:1, one launch (start us, length us, event | category | flops | bytes accessed | tf_op | source)
XLA Modules:
  0.0 83.8 jit_solution(11949163075734220728)
XLA Ops:
  0.6 8.7 %collective-permute-start = (f32[2048,128]{1,0:T(8,128)}, f32[2048,128]{1,0:T(8,128)S(1)}, u32[]{:S(2)}, u32[]{:S(2)}) collective-permute-start(f32[2048,128]{1,0:T(8,128)} %own.3), channel_id=1, source_target_pairs={{0,1},{1,0},{2,3},{3,2},{4,5},{5,4},{6,7},{7,6},{8,9},{9,8},{10,11... | collective-permute-start | bytes 3145736 | tf_op jit(solution)/shard_map/ppermute | solution.py:440
  9.4 2.9 %pick.1 = (f32[32,8,192]{2,1,0:T(8,128)}, f32[8,256]{1,0:T(8,128)S(1)}, s32[1]{0:T(128)}) custom-call(s32[1,256]{1,0:T(1,128)} %bitcast.7, f32[2048,128]{1,0:T(8,128)} %own.3, f32[64,2048]{1,0:T(8,128)} %bitcast.5), custom_call_target="tpu_custom_call" | custom-call | tf_op jit(solution)/shard_map/pick/pallas_call | solution.py:330
  12.3 4.3 %all-to-all-start.3 = ((f32[32,8,192]{2,1,0:T(8,128)}), f32[32,8,192]{2,1,0:T(8,128)S(1)}, u32[]{:S(2)}, u32[]{:S(2)}) async-start(f32[32,8,192]{2,1,0:T(8,128)} %get-tuple-element.33), calls=%async_computation.3 | async-start | bytes 524288 | tf_op jit(solution)/shard_map/all_to_all | solution.py:439
  17.3 9.6 %all-to-all-done.3 = f32[32,8,192]{2,1,0:T(8,128)S(1)} async-done(((f32[32,8,192]{2,1,0:T(8,128)}), f32[32,8,192]{2,1,0:T(8,128)S(1)}, u32[]{:S(2)}, u32[]{:S(2)}) %all-to-all-start.3) | async-done | bytes 196640 | tf_op jit(solution)/shard_map/all_to_all | solution.py:439
  26.9 0.0 copy-start
  26.9 0.0 copy-start.1
  26.9 22.3 %conditional.1 = ((f32[256,128]{1,0:T(8,128)S(1)}, f32[256,64]{1,0:T(8,128)S(1)})) conditional(s32[]{:T(128)} %bitcast.2, (f32[32,8,192]{2,1,0:T(8,128)S(1)}, f32[8,256]{1,0:T(8,128)S(1)}) %tuple.17, (f32[32,8,192]{2,1,0:T(8,128)S(1)}, f32[8,256]{1,0:T(8,128)S(1)}) %tuple.17, (f32[32,8,192]{2,1,0:T(8,128)S(1)}, ...), branch_computations={%region_0.0_spmd, %region_1.0_spmd, %region_2.0_spmd} | conditional | bytes 3145736 | solution.py:445
  26.9 0.5 branch_1_fun.2
  27.4 21.4 %all_to_all.23.received = f32[8,96,128]{2,1,0:T(8,128)S(1)} all-to-all(f32[8,96,128]{2,1,0:T(8,128)S(1)} %branch_1_fun.2), channel_id=1, replica_groups=mesh['rows_0'=8,'rows_1'=4,'rows_2'=8,'modes'=2] {'rows_0'}, dimensions={0} | all-to-all | bytes 786432 | tf_op jit(solution)/shard_map/cond/branch_1_fun/all_to_all | solution.py:410
  48.7 0.5 branch_1_fun.3
  49.2 5.8 %all_gather.3.sampled = f32[256,256]{1,0:T(8,128)S(1)} all-gather(f32[256,128]{1,0:T(8,128)S(1)} %get-tuple-element.35), channel_id=1, replica_groups=mesh['rows_0'=8,'rows_1'=4,'rows_2'=8,'modes'=2] {'modes'}, dimensions={1}, use_global_device_ids=true | all-gather | bytes 393216 | tf_op jit(solution)/shard_map/all_gather | solution.py:446
  55.0 0.0 collective-permute-done.other
  55.0 0.0 copy-done
  55.0 0.0 copy-done.1
  55.0 5.0 %fit.1 = (f32[64,2048]{1,0:T(8,128)S(1)}, f32[256,1,64]{2,1,0:T(1,128)}, f32[256,256]{1,0:T(8,128)}, bf16[256,256]{1,0:T(8,128)(2,1)S(1)}) custom-call(f32[256,256]{1,0:T(8,128)S(1)} %all_gather.3.sampled, f32[256,64]{1,0:T(8,128)S(1)} %get-tuple-element.36.shots, f32[2048,128]{1,0:T(8,128)S(1)} %copy-done, f32[2048,128]{1,0:T(8,128)S(1)} %collective-permute-done.other, ...), custom_call_target="tpu_custom_call" | custom-call | flops 402653184 | bytes 4194304 | tf_op jit(solution)/shard_map/fit/pallas_call | solution.py:170
  60.0 10.8 %all-to-all-start.4 = ((f32[256,1,64]{2,1,0:T(1,128)}), f32[256,1,64]{2,1,0:T(1,128)S(1)}, u32[]{:S(2)}, u32[]{:S(2)}) async-start(f32[256,1,64]{2,1,0:T(1,128)} %get-tuple-element.42), calls=%async_computation.4 | async-start | bytes 262144 | tf_op jit(solution)/shard_map/all_to_all | solution.py:432
  70.8 0.0 copy-start.2
  70.8 0.9 %copy-done.2 = f32[256,256]{1,0:T(8,128)S(1)} copy-done((f32[256,256]{1,0:T(8,128)S(1)}, f32[256,256]{1,0:T(8,128)}, u32[]{:S(2)}) %copy-start.2) | copy-done | bytes 262168
  71.8 4.6 %project.1 = (f32[2048,128]{1,0:T(8,128)}, f32[64,2048]{1,0:T(8,128)}) custom-call(f32[256,256]{1,0:T(8,128)S(1)} %copy-done.2, bf16[256,256]{1,0:T(8,128)(2,1)S(1)} %get-tuple-element.38.guess, f32[2048,128]{1,0:T(8,128)S(1)} %copy-done, f32[2048,128]{1,0:T(8,128)S(1)} %collective-permute-done.other, f32[64,2048]{1,0:T(8,128)S(1)} %get-tuple-element.39.residual), custom_call_target="tpu_custom_call" | custom-call | flops 805306368 | bytes 3145728 | tf_op jit(solution)/shard_map/project/pallas_call | solution.py:229
  76.4 6.6 %all-to-all-done.4.squares = f32[256,1,64]{2,1,0:T(1,128)S(1)} async-done(((f32[256,1,64]{2,1,0:T(1,128)}), f32[256,1,64]{2,1,0:T(1,128)S(1)}, u32[]{:S(2)}, u32[]{:S(2)}) %all-to-all-start.4) | async-done | bytes 65568 | tf_op jit(solution)/shard_map/all_to_all | solution.py:432
  83.0 0.8 root_mean.1
Async XLA Ops:
  0.6 54.4 %collective-permute-start = (f32[2048,128]{1,0:T(8,128)}, f32[2048,128]{1,0:T(8,128)S(1)}, u32[]{:S(2)}, u32[]{:S(2)}) collective-permute-start(f32[2048,128]{1,0:T(8,128)} %own.3), channel_id=1, source_target_pairs={{0,1},{1,0},{2,3},{3,2},{4,5},{5,4},{6,7},{7,6},{8,9},{9,8},{10,11... | collective-permute-start | bytes 3145736 | tf_op jit(solution)/shard_map/ppermute | solution.py:440
  12.3 14.6 %all-to-all-start.3 = ((f32[32,8,192]{2,1,0:T(8,128)}), f32[32,8,192]{2,1,0:T(8,128)S(1)}, u32[]{:S(2)}, u32[]{:S(2)}) async-start(f32[32,8,192]{2,1,0:T(8,128)} %get-tuple-element.33), calls=%async_computation.3 | async-start | bytes 524288 | tf_op jit(solution)/shard_map/all_to_all | solution.py:439
  26.9 28.1 %copy-start = (f32[2048,128]{1,0:T(8,128)S(1)}, f32[2048,128]{1,0:T(8,128)}, u32[]{:S(2)}) copy-start(f32[2048,128]{1,0:T(8,128)} %own.3) | copy-start | bytes 3145732
  26.9 28.1 %copy-start.1 = (f32[2048,64]{0,1:T(8,128)S(1)}, f32[2048,64]{0,1:T(8,128)}, u32[]{:S(2)}) copy-start(f32[2048,64]{0,1:T(8,128)} %param.8) | copy-start | bytes 1572868
  60.0 22.9 %all-to-all-start.4 = ((f32[256,1,64]{2,1,0:T(1,128)}), f32[256,1,64]{2,1,0:T(1,128)S(1)}, u32[]{:S(2)}, u32[]{:S(2)}) async-start(f32[256,1,64]{2,1,0:T(1,128)} %get-tuple-element.42), calls=%async_computation.4 | async-start | bytes 262144 | tf_op jit(solution)/shard_map/all_to_all | solution.py:432
  70.8 1.0 %copy-start.2 = (f32[256,256]{1,0:T(8,128)S(1)}, f32[256,256]{1,0:T(8,128)}, u32[]{:S(2)}) copy-start(f32[256,256]{1,0:T(8,128)} %get-tuple-element.37.system) | copy-start | bytes 786436

commit v7 on v6

--- a/solution.py
+++ b/solution.py
@@ -78,44 +78,59 @@
     return guess.astype(BF16)
 
 
-def shrinks(scaled, guess):
-    product = None
-    rest = scaled
-    for _ in range(3):
-        piece = rest.astype(BF16)
-        rest = rest - piece.astype(F32)
-        part = jnp.dot(guess, piece, preferred_element_type=F32)
-        product = part if product is None else product + part
-    gap = jnp.where(diagonal_of(scaled.shape), 1.0, 0.0) - product
-    gap = jnp.sum(jnp.abs(gap), axis=1, keepdims=True)
-    rounding = jnp.sum(jnp.abs(guess.astype(F32)), axis=1, keepdims=True) * 2.0**-8
-    return jnp.max(gap + rounding) <= SHRINK
-
-
-def refine(scaled, guess, right):
-    out = jnp.dot(guess, right.astype(BF16), preferred_element_type=F32)
-    for _ in range(REFINES):
-        left = (right - dot_full(scaled, out)).astype(BF16)
-        out = out + jnp.dot(guess, left, preferred_element_type=F32)
-    return out
-
-
-def solve(scaled, guess, right, matrix, answer):
-    answer[...] = refine(scaled, guess, right)
-
-    @pl.when(jnp.logical_not(shrinks(scaled, guess)))
-    def _():
-        matrix[...] = scaled
-        answer[...] = right
-        eliminate(matrix, answer)
-
-
 def pieces_of(values):
     pieces = []
     for _ in range(3):
         pieces.append(values.astype(BF16))
         values = values - pieces[-1].astype(F32)
     return pieces
+
+
+def dot_pieces(lefts, rights):
+    total = None
+    for left in lefts:
+        part = jnp.dot(left, rights, preferred_element_type=F32)
+        total = part if total is None else total + part
+    return total
+
+
+def folded(product):
+    width = product.shape[1] // 3
+    low = product[:, 2 * width :]
+    pair = product[:, : 2 * width] + jnp.concatenate([low, jnp.zeros_like(low)], axis=1)
+    return pair[:, :width] + pair[:, width:]
+
+
+def shrinks(pieces, guess):
+    product = None
+    for piece in pieces:
+        part = jnp.dot(guess, piece, preferred_element_type=F32)
+        product = part if product is None else product + part
+    gap = jnp.where(diagonal_of(guess.shape), 1.0, 0.0) - product
+    gap = jnp.sum(jnp.abs(gap), axis=1, keepdims=True)
+    rounding = jnp.sum(jnp.abs(guess.astype(F32)), axis=1, keepdims=True) * 2.0**-8
+    return jnp.max(gap + rounding) <= SHRINK
+
+
+def refine(pieces, guess, right):
+    out = jnp.dot(guess, right.astype(BF16), preferred_element_type=F32)
+    for _ in range(REFINES):
+        spread = jnp.concatenate(pieces_of(out), axis=1)
+        left = (right - folded(dot_pieces(pieces, spread))).astype(BF16)
+        out = out + jnp.dot(guess, left, preferred_element_type=F32)
+    return out
+
+
+def solve(scaled, guess, right, matrix, answer):
+    pieces = pieces_of(scaled)
+    sure = shrinks(pieces, guess)
+    answer[...] = refine(pieces, guess, right)
+
+    @pl.when(jnp.logical_not(sure))
+    def _():
+        matrix[...] = scaled
+        answer[...] = right
+        eliminate(matrix, answer)
 
 
 def own_first(answer):
@@ -249,7 +264,50 @@
     )(system, guess, own, other, residual)
 
 
-def pick_body(sizes, wanted, basis, snaps, sends, places, crowded, blocks, strips, sem):
+def counter(key):
+    count = key.shape[1]
+    across = jnp.broadcast_to(key.astype(F32), (count, count))
+    down = across.T
+    before = down < across
+
+    def earlier(first):
+        same = before & (down >= first.astype(F32))
+        return jnp.sum(jnp.where(same, 1.0, 0.0), axis=0, keepdims=True)
+
+    return earlier
+
+
+def plan_body(rows, deep, wanted, places, crowded):
+    key = wanted[...]
+    slab = key // rows
+    plane = slab // deep
+    line = slab % deep
+    earlier = counter(key)
+    place = earlier(plane * deep * rows)
+    slot = (line * MOST).astype(F32) + earlier(slab * rows)
+    empty = jnp.zeros((8 - 3, key.shape[1]), F32)
+    places[...] = jnp.concatenate([place, plane.astype(F32), slot, empty], axis=0)
+    most = jnp.max(place)
+    crowded[0] = sum((most >= room).astype(jnp.int32) for room in ROOMS)
+
+
+def plan(sizes, rows, wanted):
+    count = wanted.shape[0]
+    inside = pl.BlockSpec(memory_space=pltpu.VMEM)
+    return pl.pallas_call(
+        functools.partial(plan_body, rows, sizes[1] * sizes[2]),
+        out_shape=(
+            jax.ShapeDtypeStruct((8, count), F32),
+            jax.ShapeDtypeStruct((1,), jnp.int32),
+        ),
+        in_specs=[inside],
+        out_specs=(inside, pl.BlockSpec(memory_space=pltpu.SMEM)),
+        compiler_params=pltpu.CompilerParams(vmem_limit_bytes=8 * 1024 * 1024),
+        name="plan",
+    )(wanted.reshape(1, count))
+
+
+def pick_body(sizes, wanted, basis, snaps, sends, blocks, strips, sem):
     rows, half = basis.shape
     shots = snaps.shape[0]
     count = wanted.shape[1]
@@ -261,18 +319,7 @@
 
     key = wanted[...]
     local = key % rows
-    slab = key // rows
-    plane = slab // deep
-    line = slab % deep
-    across = jnp.broadcast_to(key.astype(F32), (count, count))
-    down = across.T
-    before = down < across
-
-    def earlier(first):
-        same = before & (down >= first.astype(F32))
-        return jnp.sum(jnp.where(same, 1.0, 0.0), axis=0, keepdims=True)
-
-    rank = earlier(key - local)
+    rank = counter(key)(key - local)
     turn = lax.broadcasted_iota(jnp.int32, (MOST, count), 0).astype(F32)
     held = (key >= start) & (key < start + rows)
     chosen = jnp.where(held & (rank == turn), local.astype(F32) + 1.0, 0.0)
@@ -293,13 +340,6 @@
         def _():
             for copy in copies(n):
                 copy.start()
-
-    place = earlier(plane * deep * rows)
-    slot = (line * MOST).astype(F32) + rank
-    empty = jnp.zeros((8 - 3, count), F32)
-    places[...] = jnp.concatenate([place, plane.astype(F32), slot, empty], axis=0)
-    most = jnp.max(place)
-    crowded[0] = sum((most >= room).astype(jnp.int32) for room in ROOMS)
 
     for n in range(MOST):
 
@@ -329,13 +369,9 @@
     inside = pl.BlockSpec(memory_space=pltpu.VMEM)
     return pl.pallas_call(
         functools.partial(pick_body, sizes),
-        out_shape=(
-            jax.ShapeDtypeStruct((sizes[1] * sizes[2], MOST, half + shots), F32),
-            jax.ShapeDtypeStruct((8, count), F32),
-            jax.ShapeDtypeStruct((1,), jnp.int32),
-        ),
+        out_shape=jax.ShapeDtypeStruct((sizes[1] * sizes[2], MOST, half + shots), F32),
         in_specs=[inside, outside, outside],
-        out_specs=(inside, inside, pl.BlockSpec(memory_space=pltpu.SMEM)),
+        out_specs=inside,
         scratch_shapes=[
             pltpu.VMEM((MOST, 8, half), F32),
             pltpu.VMEM((MOST, shots, 128), F32),
@@ -435,8 +471,9 @@
 def on_device(sizes, sample_rows, basis, snapshots):
     snaps = snapshots.T
     half = basis.shape[1]
-    sends, places, crowded = pick(sizes, sample_rows, basis, snaps)
+    sends = pick(sizes, sample_rows, basis, snaps)
     gathered = lax.all_to_all(sends, ROWS[1:], 0, 0, tiled=True)
+    places, crowded = plan(sizes, basis.shape[0], sample_rows)
     other = lax.ppermute(basis, "modes", [(0, 1), (1, 0)])
     branches = [
         functools.partial(along_planes, sizes[0], half, room)

time: 84.2 us -> 83.8 us (level)
    pallas_call x1 -> x2, Pallas kernels: 2.87 us -> 3.62 us  [the longest x1 2.83 us: pick(): pl.pallas_call(functools.partial(pick_body, sizes), out_shape=jax.ShapeDt...]
where the time goes in v7:
time: 83.8 us; the launch traced here: 83.4 us
  blocking collectives  27.2 us (32%)
  starting transfers between devices  23.7 us (28%)
  waiting for transfers between devices  16.1 us (19%)
  Pallas kernels  14.1 us (17%)
  between operations  1.37 us (2%)
  local copies, waits for them, and re-layouts  0.96 us (1%)
    all_to_all x1, blocking collectives, along_planes(): received = lax.all_to_all(sends, ROWS[0], 0, 0, tiled=True)  21.4 us
    all_to_all x1, starting transfers between devices, exchange(): return lax.all_to_all(blocks, ROWS, 0, 0, tiled=True)  10.6 us
    all_to_all x1, waiting for transfers between devices, on_device(): gathered = lax.all_to_all(sends, ROWS[1:], 0, 0, tiled=True)  8.83 us
    ppermute x1, starting transfers between devices, on_device(): other = lax.ppermute(basis, 'modes', [(0, 1), (1, 0)])  8.75 us
    all_to_all x1, waiting for transfers between devices, exchange(): return lax.all_to_all(blocks, ROWS, 0, 0, tiled=True)  7.25 us
    all_gather x1, blocking collectives, on_device(): sampled = lax.all_gather(modes, 'modes', axis=1, tiled=True)  5.78 us
    pallas_call x1, Pallas kernels, fit(): pl.pallas_call(fit_body, out_shape=(jax.ShapeDtypeStruct((depth, rows), F...  4.65 us
    all_to_all x1, starting transfers between devices, on_device(): gathered = lax.all_to_all(sends, ROWS[1:], 0, 0, tiled=True)  4.34 us
  transfers between devices with their start and end apart: 3, of which 2 were waited for; matrix products, arithmetic and copies ran while one was open for 0% of the time, Pallas kernels for 10%

profile of v7, /device:TPU:1, one launch (start us, length us, event | category | flops | bytes accessed | tf_op | source)
XLA Modules:
  0.0 83.4 jit_solution(4925982263393014508)
XLA Ops:
  0.6 0.0 copy-start.3
  0.6 8.7 %collective-permute-start = (f32[2048,128]{1,0:T(8,128)}, f32[2048,128]{1,0:T(8,128)S(1)}, u32[]{:S(2)}, u32[]{:S(2)}) collective-permute-start(f32[2048,128]{1,0:T(8,128)} %own.3), channel_id=1, source_target_pairs={{0,1},{1,0},{2,3},{3,2},{4,5},{5,4},{6,7},{7,6},{8,9},{9,8},{10,11... | collective-permute-start | bytes 3145736 | tf_op jit(solution)/shard_map/ppermute | solution.py:477
  9.4 2.8 %pick.1 = f32[32,8,192]{2,1,0:T(8,128)} custom-call(s32[1,256]{1,0:T(1,128)} %bitcast.7, f32[2048,128]{1,0:T(8,128)} %own.3, f32[64,2048]{1,0:T(8,128)} %bitcast.5), custom_call_target="tpu_custom_call" | custom-call | tf_op jit(solution)/shard_map/pick/pallas_call | solution.py:370
  12.2 4.3 %all-to-all-start.3 = ((f32[32,8,192]{2,1,0:T(8,128)}), f32[32,8,192]{2,1,0:T(8,128)S(1)}, u32[]{:S(2)}, u32[]{:S(2)}) async-start(f32[32,8,192]{2,1,0:T(8,128)} %pick.1), calls=%async_computation.3 | async-start | bytes 524288 | tf_op jit(solution)/shard_map/all_to_all | solution.py:475
  16.6 0.0 copy-done.3
  16.6 0.8 plan.1
  18.0 8.8 %all-to-all-done.3 = f32[32,8,192]{2,1,0:T(8,128)S(1)} async-done(((f32[32,8,192]{2,1,0:T(8,128)}), f32[32,8,192]{2,1,0:T(8,128)S(1)}, u32[]{:S(2)}, u32[]{:S(2)}) %all-to-all-start.3) | async-done | bytes 196640 | tf_op jit(solution)/shard_map/all_to_all | solution.py:475
  26.9 0.0 copy-start
  26.9 0.0 copy-start.1
  26.9 22.3 %conditional.1 = ((f32[256,128]{1,0:T(8,128)S(1)}, f32[256,64]{1,0:T(8,128)S(1)})) conditional(s32[]{:T(128)} %bitcast.1, (f32[32,8,192]{2,1,0:T(8,128)S(1)}, f32[8,256]{1,0:T(8,128)S(1)}) %tuple.17, (f32[32,8,192]{2,1,0:T(8,128)S(1)}, f32[8,256]{1,0:T(8,128)S(1)}) %tuple.17, (f32[32,8,192]{2,1,0:T(8,128)S(1)}, ...), branch_computations={%region_0.0_spmd, %region_1.0_spmd, %region_2.0_spmd} | conditional | bytes 3145736 | solution.py:482
  26.9 0.5 branch_1_fun.2
  27.3 21.4 %all_to_all.23.received = f32[8,96,128]{2,1,0:T(8,128)S(1)} all-to-all(f32[8,96,128]{2,1,0:T(8,128)S(1)} %branch_1_fun.2), channel_id=1, replica_groups=mesh['rows_0'=8,'rows_1'=4,'rows_2'=8,'modes'=2] {'rows_0'}, dimensions={0} | all-to-all | bytes 786432 | tf_op jit(solution)/shard_map/cond/branch_1_fun/all_to_all | solution.py:446
  48.7 0.5 branch_1_fun.3
  49.2 5.8 %all_gather.3.sampled = f32[256,256]{1,0:T(8,128)S(1)} all-gather(f32[256,128]{1,0:T(8,128)S(1)} %get-tuple-element.33), channel_id=1, replica_groups=mesh['rows_0'=8,'rows_1'=4,'rows_2'=8,'modes'=2] {'modes'}, dimensions={1}, use_global_device_ids=true | all-gather | bytes 393216 | tf_op jit(solution)/shard_map/all_gather | solution.py:483
  55.0 0.0 collective-permute-done.other
  55.0 0.0 copy-done
  55.0 0.0 copy-done.1
  55.0 4.6 %fit.1 = (f32[64,2048]{1,0:T(8,128)S(1)}, f32[256,1,64]{2,1,0:T(1,128)}, f32[256,256]{1,0:T(8,128)}, bf16[256,256]{1,0:T(8,128)(2,1)S(1)}) custom-call(f32[256,256]{1,0:T(8,128)S(1)} %all_gather.3.sampled, f32[256,64]{1,0:T(8,128)S(1)} %get-tuple-element.34.shots, f32[2048,128]{1,0:T(8,128)S(1)} %copy-done, f32[2048,128]{1,0:T(8,128)S(1)} %collective-permute-done.other, ...), custom_call_target="tpu_custom_call" | custom-call | flops 402653184 | bytes 4194304 | tf_op jit(solution)/shard_map/fit/pallas_call | solution.py:185
  59.7 10.6 %all-to-all-start.4 = ((f32[256,1,64]{2,1,0:T(1,128)}), f32[256,1,64]{2,1,0:T(1,128)S(1)}, u32[]{:S(2)}, u32[]{:S(2)}) async-start(f32[256,1,64]{2,1,0:T(1,128)} %get-tuple-element.40), calls=%async_computation.4 | async-start | bytes 262144 | tf_op jit(solution)/shard_map/all_to_all | solution.py:468
  70.3 0.0 copy-start.2
  70.3 0.9 %copy-done.2 = f32[256,256]{1,0:T(8,128)S(1)} copy-done((f32[256,256]{1,0:T(8,128)S(1)}, f32[256,256]{1,0:T(8,128)}, u32[]{:S(2)}) %copy-start.2) | copy-done | bytes 262168
  71.2 4.1 %project.1 = (f32[2048,128]{1,0:T(8,128)}, f32[64,2048]{1,0:T(8,128)}) custom-call(f32[256,256]{1,0:T(8,128)S(1)} %copy-done.2, bf16[256,256]{1,0:T(8,128)(2,1)S(1)} %get-tuple-element.36.guess, f32[2048,128]{1,0:T(8,128)S(1)} %copy-done, f32[2048,128]{1,0:T(8,128)S(1)} %collective-permute-done.other, f32[64,2048]{1,0:T(8,128)S(1)} %get-tuple-element.37.residual), custom_call_target="tpu_custom_call" | custom-call | flops 805306368 | bytes 3145728 | tf_op jit(solution)/shard_map/project/pallas_call | solution.py:244
  75.3 7.3 %all-to-all-done.4.squares = f32[256,1,64]{2,1,0:T(1,128)S(1)} async-done(((f32[256,1,64]{2,1,0:T(1,128)}), f32[256,1,64]{2,1,0:T(1,128)S(1)}, u32[]{:S(2)}, u32[]{:S(2)}) %all-to-all-start.4) | async-done | bytes 65568 | tf_op jit(solution)/shard_map/all_to_all | solution.py:468
  82.6 0.8 root_mean.1
Async XLA Ops:
  0.6 16.0 %copy-start.3 = (s32[256]{0:T(256)S(1)}, s32[256]{0:T(256)}, u32[]{:S(2)}) copy-start(s32[256]{0:T(256)} %param.6) | copy-start | bytes 3076
  0.6 54.4 %collective-permute-start = (f32[2048,128]{1,0:T(8,128)}, f32[2048,128]{1,0:T(8,128)S(1)}, u32[]{:S(2)}, u32[]{:S(2)}) collective-permute-start(f32[2048,128]{1,0:T(8,128)} %own.3), channel_id=1, source_target_pairs={{0,1},{1,0},{2,3},{3,2},{4,5},{5,4},{6,7},{7,6},{8,9},{9,8},{10,11... | collective-permute-start | bytes 3145736 | tf_op jit(solution)/shard_map/ppermute | solution.py:477
  12.2 14.6 %all-to-all-start.3 = ((f32[32,8,192]{2,1,0:T(8,128)}), f32[32,8,192]{2,1,0:T(8,128)S(1)}, u32[]{:S(2)}, u32[]{:S(2)}) async-start(f32[32,8,192]{2,1,0:T(8,128)} %pick.1), calls=%async_computation.3 | async-start | bytes 524288 | tf_op jit(solution)/shard_map/all_to_all | solution.py:475
  26.9 28.1 %copy-start = (f32[2048,128]{1,0:T(8,128)S(1)}, f32[2048,128]{1,0:T(8,128)}, u32[]{:S(2)}) copy-start(f32[2048,128]{1,0:T(8,128)} %own.3) | copy-start | bytes 3145732
  26.9 28.1 %copy-start.1 = (f32[2048,64]{0,1:T(8,128)S(1)}, f32[2048,64]{0,1:T(8,128)}, u32[]{:S(2)}) copy-start(f32[2048,64]{0,1:T(8,128)} %param.8) | copy-start | bytes 1572868
  59.7 22.9 %all-to-all-start.4 = ((f32[256,1,64]{2,1,0:T(1,128)}), f32[256,1,64]{2,1,0:T(1,128)S(1)}, u32[]{:S(2)}, u32[]{:S(2)}) async-start(f32[256,1,64]{2,1,0:T(1,128)} %get-tuple-element.40), calls=%async_computation.4 | async-start | bytes 262144 | tf_op jit(solution)/shard_map/all_to_all | solution.py:468
  70.3 1.0 %copy-start.2 = (f32[256,256]{1,0:T(8,128)S(1)}, f32[256,256]{1,0:T(8,128)}, u32[]{:S(2)}) copy-start(f32[256,256]{1,0:T(8,128)} %get-tuple-element.35.system) | copy-start | bytes 786436
